TPU v7x, 32 devices: a whole 2x2x4 slice. The times are simulated.
32 devices in a mesh: cp: 4 (over z), tp: 8 (over y, x, core).
Axes of the slice: x: 2, y: 2, z: 4, core: 2. Of those that a mesh axis runs over, the one named last changes fastest.
Arguments:
- checkpoint: bfloat16 [2048, 8192], P('cp', 'tp'), may hold values from -6 to 6
- norm_gain: float32 [8192], replicated, may hold values from 0.1 to 1.9
- query_weight: bfloat16 [8192, 8192], P(None, 'tp'), may hold values from -4 to 4
- key_weight: bfloat16 [8192, 1024], P(None, 'tp'), may hold values from -1 to 1
- value_weight: bfloat16 [8192, 1024], P(None, 'tp'), may hold values from -0.0625 to 0.0625
- output_weight: bfloat16 [8192, 8192], P('tp'), may hold values from -0.09375 to 0.09375
- block_order: int32 [8], replicated, may hold values from 0 to 7, each once
Outputs:
- projected: bfloat16 [2048, 8192], P('cp', 'tp')
- log_normalizer: float32 [64, 2048], P('tp', 'cp')
Inputs may be any that keep to these rules, and one draw needn't show every extreme that they name: `block_order`: each of 0 to 7 once.
All inputs are finite; a program needn't handle non-finite values.
Results may differ from a plain program's by a relative error of at most 0.019.
Values may be sent and summed in bfloat16 or wider, within the bound.
No kernel may reach another device: no remote copies, remote signals or barrier semaphores. Data moves between devices by JAX's collectives and lax.ppermute only.
A program may use at most 128 MiB of HBM per device.

v0:
```python
import math

import jax
import jax.numpy as jnp
from jax import lax
from jax.sharding import PartitionSpec as P

KV_HEADS = 8
HEAD_DIM = 128


rope_base = 500000.0
norm_epsilon = 1e-05
masked_score = -1e30


def partner_2(block, axis, stride):
    count = lax.axis_size(axis)
    route = []
    for low in range(count):
        high = low | 1 << stride
        if high != low and high < count:
            route += [(low, high), (high, low)]
    return lax.ppermute(block, axis, route)


def from_behind(block, axis, distance):
    devices = range(lax.axis_size(axis))
    route = [((i - distance) % len(devices), i) for i in devices]
    return lax.ppermute(block, axis, route)


def turn_pairs(matrix, positions, first_pair):
    pair_count = matrix.shape[-1] // 2
    pair_index = (first_pair + jnp.arange(pair_count, dtype=jnp.int32)).astype(jnp.float32)
    inverse_rates = rope_base ** (-2.0 * pair_index / HEAD_DIM)
    angles = positions.astype(jnp.float32)[:, None] * inverse_rates[None, :]
    cosine = jnp.cos(angles)[:, None, :]
    sine_part = jnp.sin(angles)[:, None, :]
    paired = matrix.reshape(matrix.shape[0], matrix.shape[1], pair_count, 2)
    former = paired[..., 0]
    latter = paired[..., 1]
    turned = jnp.stack(
        [former * cosine - latter * sine_part, former * sine_part + latter * cosine], axis=-1
    )
    return turned.reshape(matrix.shape)


def shards(
    checkpoint, norm_gain, query_weight, key_weight, value_weight, output_weight, block_order
):
    tok_rows = checkpoint.shape[0]
    block_rows = tok_rows // 2
    local_heads = query_weight.shape[1] // HEAD_DIM
    key_columns = key_weight.shape[1]
    context_rank = lax.axis_index("cp")
    tensor_rank = lax.axis_index("tp")
    row_offsets = jnp.arange(block_rows, dtype=jnp.int32)
    own_blocks = lax.dynamic_slice_in_dim(block_order, 2 * context_rank, 2)
    own_positions = (own_blocks[:, None] * block_rows + row_offsets[None, :]).reshape(tok_rows)
    gathered = lax.all_gather(checkpoint, "tp", axis=1, tiled=True)
    widened = gathered.astype(jnp.float32)
    mean_square = jnp.mean(widened * widened, axis=-1, keepdims=True)
    normed = (widened * lax.rsqrt(mean_square + norm_epsilon) * norm_gain).astype(jnp.bfloat16)
    query_features = jnp.dot(normed, query_weight, preferred_element_type=jnp.float32)
    key_features = jnp.dot(normed, key_weight, preferred_element_type=jnp.float32)
    value_features = jnp.dot(normed, value_weight, preferred_element_type=jnp.float32)
    queries = turn_pairs(
        query_features.reshape(tok_rows, local_heads, HEAD_DIM), own_positions, 0
    ).astype(jnp.bfloat16)
    sharing = lax.axis_size("tp") // KV_HEADS
    part_of_head = tensor_rank % sharing
    key_part = turn_pairs(
        key_features.reshape(tok_rows, 1, key_columns),
        own_positions,
        part_of_head * (key_columns // 2),
    )
    key_part = key_part.astype(jnp.bfloat16).reshape(tok_rows, key_columns)
    value_part = value_features.astype(jnp.bfloat16)
    own_pair = jnp.stack([key_part, value_part])
    if sharing == 2:
        partner = partner_2(own_pair, "tp", 0)
        lower_first = jnp.concatenate([own_pair, partner], axis=-1)
        upper_first = jnp.concatenate([partner, own_pair], axis=-1)
        key_value = jnp.where(part_of_head == 0, lower_first, upper_first)
    else:
        key_value = own_pair
    score_scale = 1.0 / math.sqrt(HEAD_DIM)

    def absorb(running, query_slot, key_block, key_rows, value_rows):
        query_block = own_blocks[query_slot]
        top_scores, totals, weighted = running
        query_rows = queries[query_slot * block_rows : (query_slot + 1) * block_rows]
        scores = (
            jnp.einsum("qhd,kd->qhk", query_rows, key_rows, preferred_element_type=jnp.float32)
            * score_scale
        )
        query_places = query_block * block_rows + row_offsets
        key_places = key_block * block_rows + row_offsets
        allowed = (key_places[None, :] <= query_places[:, None])[:, None, :]
        scores = jnp.where(allowed, scores, masked_score)
        old_top = top_scores[query_slot]
        new_top = jnp.maximum(old_top, jnp.max(scores, axis=-1))
        weights = jnp.where(allowed, jnp.exp(scores - new_top[..., None]), 0.0)
        shrink = jnp.exp(old_top - new_top)
        new_total = totals[query_slot] * shrink + jnp.sum(weights, axis=-1)
        new_sum = weighted[query_slot] * shrink[..., None] + jnp.einsum(
            "qhk,kd->qhd",
            weights.astype(jnp.bfloat16),
            value_rows,
            preferred_element_type=jnp.float32,
        )
        return (
            top_scores.at[query_slot].set(new_top),
            totals.at[query_slot].set(new_total),
            weighted.at[query_slot].set(new_sum),
        )

    def visit_rows(running, key_value_rows, first_row):
        block_count = key_value_rows.shape[1] // block_rows

        def one_block(block_index, current):
            rows_here = lax.dynamic_slice_in_dim(
                key_value_rows, block_index * block_rows, block_rows, 1
            )
            stored = first_row // block_rows + block_index
            key_block = lax.dynamic_index_in_dim(block_order, stored, 0, keepdims=False)
            for query_slot in range(2):
                current = absorb(current, query_slot, key_block, rows_here[0], rows_here[1])
            return current

        return lax.fori_loop(0, block_count, one_block, running)

    running = (
        jnp.full((2, block_rows, local_heads), masked_score, jnp.float32),
        jnp.zeros((2, block_rows, local_heads), jnp.float32),
        jnp.zeros((2, block_rows, local_heads, HEAD_DIM), jnp.float32),
    )
    running = visit_rows(running, key_value, context_rank * tok_rows)
    context_size = lax.axis_size("cp")

    def pass_turn(turn_index, carried):
        current, travelling = carried
        travelling = from_behind(travelling, "cp", 1)
        source = (context_rank - turn_index) % context_size
        return (visit_rows(current, travelling, source * tok_rows), travelling)

    running, unused = lax.fori_loop(1, context_size, pass_turn, (running, key_value))
    top_scores, totals, weighted = running
    attended = (
        (weighted / totals[..., None])
        .astype(jnp.bfloat16)
        .reshape(tok_rows, local_heads * HEAD_DIM)
    )
    normalizer = jnp.transpose((top_scores + jnp.log(totals)).reshape(tok_rows, local_heads))
    partial_terms = jnp.dot(attended, output_weight, preferred_element_type=jnp.float32)
    projected = lax.psum_scatter(
        partial_terms.astype(jnp.bfloat16), "tp", scatter_dimension=1, tiled=True
    )
    return (projected, normalizer)


def solution(mesh):
    return jax.shard_map(
        shards,
        mesh=mesh,
        in_specs=(
            P("cp", "tp"),
            P(),
            P(None, "tp"),
            P(None, "tp"),
            P(None, "tp"),
            P("tp", None),
            P(),
        ),
        out_specs=(P("cp", "tp"), P("tp", "cp")),
        check_vma=False,
    )
```

profile of v0, /device:TPU:0, one launch (start us, length us, event | category | flops | bytes accessed | tf_op | source)
XLA Modules:
  0.0 284.2 jit_solution(17932145199853954866)
XLA Ops:
  7.2 0.7 all-gather.2.cloned.1.call-update
  8.0 0.7 broadcast_multiply_fusion
  8.7 0.6 fusion.112
  10.6 0.5 multiply_cosine_fusion
  11.1 55.8 %all-gather.2.cloned.1.call-done = bf16[512,8192]{1,0:T(8,128)(2,1)} async-done(((bf16[512,1024]{1,0:T(8,128)(2,1)}), bf16[512,8192]{1,0:T(8,128)(2,1)}) %all-gather.2.cloned.1.call-update) | async-done | bytes 8388624 | tf_op jit(solution)/shard_map/all_gather | solution.py:61
  66.9 5.1 %fusion.92 = f32[512]{0:T(512)S(1)} fusion(bf16[512,8192]{1,0:T(8,128)(2,1)} %all-gather.2.cloned.1.call-done), kind=kLoop, calls=%fused_computation.134 | loop fusion | flops 12582400 | bytes 8390656 | tf_op jit(solution)/shard_map/reduce_sum | solution.py:63
  72.0 15.5 %fusion.106 = f32[512,1024]{0,1:T(8,128)} fusion(bf16[8192,1024]{1,0:T(8,128)(2,1)} %param.39, bf16[512,8192]{1,0:T(8,128)(2,1)} %all-gather.2.cloned.1.call-done, f32[8192]{0:T(1024)S(1)} %copy-done.5, f32[512]{0:T(512)S(1)} %add_rsqrt_fusion), kind=kOutput, calls=%fused_computation.165 | convolution fusion | flops 8606711808 | bytes 27297792 | tf_op jit(solution)/shard_map/dot_general | solution.py:65
  87.6 3.5 %reshape_reshape.7 = f32[512,8,64,2]{0,3,2,1:T(2,128)} reshape(f32[512,1024]{0,1:T(8,128)} %fusion.106) | data formatting | bytes 4194304 | tf_op jit(solution)/shard_map/reshape;reshape | solution.py:40
  91.0 5.8 %fusion.109 = f32[512,128]{0,1:T(8,128)S(1)} fusion(bf16[8192,128]{1,0:T(8,128)(2,1)S(1)} %copy-done, bf16[512,8192]{1,0:T(8,128)(2,1)} %all-gather.2.cloned.1.call-done, f32[8192]{0:T(1024)S(1)} %copy-done.5, f32[512]{0:T(512)S(1)} %add_rsqrt_fusion), kind=kOutput, calls=%fused_computation.166 | convolution fusion | flops 1090519040 | bytes 10782720 | tf_op jit(solution)/shard_map/dot_general | solution.py:66
  97.2 0.6 fusion.103
  98.4 2.9 %subtract_convert_fusion = (bf16[512,8,64,1]{0,3,2,1:T(2,128)(2,1)S(1)}, bf16[512,8,64,1]{0,3,2,1:T(2,128)(2,1)S(1)}) fusion(f32[512,8,64,2]{0,3,2,1:T(2,128)S(1)} %copy-done.2, f32[512,64]{0,1:T(8,128)S(1)} %get-tuple-element.1680, f32[512,64]{0,1:T(8,128)S(1)} %get-tuple-element.1679), kind=kLoop, calls=%fused_computation.145 | loop fusion | flops 2097152 | bytes 3407872 | tf_op jit(solution)/shard_map/convert
  101.3 2.2 pad_maximum_fusion
  103.5 1.1 copy.45
  104.7 1.2 copy.46
  105.9 6.4 %fusion.95 = bf16[1,512,128]{2,1,0:T(8,128)(2,1)S(1)} fusion(bf16[8192,128]{1,0:T(8,128)(2,1)} %param.41, bf16[512,8192]{1,0:T(8,128)(2,1)} %all-gather.2.cloned.1.call-done, f32[8192]{0:T(1024)S(1)} %copy-done.5, f32[512]{0:T(512)S(1)} %add_rsqrt_fusion), kind=kOutput, calls=%fused_computation.140 | convolution fusion | flops 1090584576 | bytes 10651648 | tf_op jit(solution)/shard_map/dot_general | solution.py:67
  112.3 0.7 pad_maximum_fusion.1
  113.2 11.7 %while.100 = (s32[]{:T(128)}, f32[2,256,8]{1,2,0:T(8,128)S(1)}, f32[2,256,8]{1,2,0:T(8,128)S(1)}, f32[2,256,8,128]{3,1,2,0:T(8,128)S(1)}, s32[]{:T(128)}, /*inde...) while((s32[]{:T(128)}, f32[2,256,8]{1,2,0:T(8,128)S(1)}, ...), condition=%wide.region_6.7_spmd.clone.clone, body=%wide.region_1.6_spmd.clone.clone.sunk | while | flops 551699200 | bytes 24107364 | solution.py:132
  113.2 0.7 dynamic_slice.54
  115.3 0.5 fusion.147
  115.9 0.9 fusion.153
  118.1 0.9 fusion.155
  119.1 0.7 dynamic_slice.54
  121.7 0.9 fusion.153
  124.0 0.9 fusion.155
  124.9 65.2 %while.102 = (s32[]{:T(128)}, f32[2,256,8]{1,2,0:T(8,128)S(1)}, f32[2,256,8]{1,2,0:T(8,128)S(1)}, f32[2,256,8,128]{3,1,2,0:T(8,128)S(1)}, bf16[2,512,128]{2,1,0:...) while((s32[]{:T(128)}, f32[2,256,8]{1,2,0:T(8,128)S(1)}, ...), condition=%wide.region_14.15_spmd.clone.clone, body=%wide.region_7.14_spmd.clone.clone.sunk | while | flops 551699200 | bytes 24634376 | solution.py:148
  124.9 1.5 collective-permute-start
  126.5 9.0 %collective-permute-done = bf16[2,512,128]{2,1,0:T(8,128)(2,1)S(1)} collective-permute-done((bf16[2,512,128]{2,1,0:T(8,128)(2,1)}, bf16[2,512,128]{2,1,0:T(8,128)(2,1)S(1)}, u32[]{:S(2)}, u32[]{:S(2)}) %collective-permute-start) | collective-permute-done | bytes 262176 | tf_op jit(solution)/shard_map/while/body/eval_jaxpr/ppermute | solution.py:30
  135.5 11.4 %while.103 = (s32[]{:T(128)}, f32[2,256,8]{1,2,0:T(8,128)S(1)}, f32[2,256,8]{1,2,0:T(8,128)S(1)}, f32[2,256,8,128]{3,1,2,0:T(8,128)S(1)}, s32[]{:T(128)}, /*inde...) while((s32[]{:T(128)}, f32[2,256,8]{1,2,0:T(8,128)S(1)}, ...), condition=%wide.region_13.13_spmd.clone, body=%wide.region_8.12_spmd.clone.sunk | while | flops 551699200 | bytes 23059792 | solution.py:132
  135.5 0.6 dynamic_slice.55
  137.9 0.9 fusion.166
  139.3 0.5 fusion.164
  140.2 0.9 fusion.168
  141.2 0.6 dynamic_slice.55
  143.7 0.9 fusion.166
  145.1 0.5 fusion.164
  145.9 0.9 fusion.168
  146.9 0.7 copy.116
  147.6 9.6 %collective-permute-done = bf16[2,512,128]{2,1,0:T(8,128)(2,1)S(1)} collective-permute-done((bf16[2,512,128]{2,1,0:T(8,128)(2,1)}, bf16[2,512,128]{2,1,0:T(8,128)(2,1)S(1)}, u32[]{:S(2)}, u32[]{:S(2)}) %collective-permute-start) | collective-permute-done | bytes 262176 | tf_op jit(solution)/shard_map/while/body/eval_jaxpr/ppermute | solution.py:30
  157.2 11.4 %while.103 = (s32[]{:T(128)}, f32[2,256,8]{1,2,0:T(8,128)S(1)}, f32[2,256,8]{1,2,0:T(8,128)S(1)}, f32[2,256,8,128]{3,1,2,0:T(8,128)S(1)}, s32[]{:T(128)}, /*inde...) while((s32[]{:T(128)}, f32[2,256,8]{1,2,0:T(8,128)S(1)}, ...), condition=%wide.region_13.13_spmd.clone, body=%wide.region_8.12_spmd.clone.sunk | while | flops 551699200 | bytes 23059792 | solution.py:132
  157.2 0.6 dynamic_slice.55
  159.7 0.9 fusion.166
  161.1 0.5 fusion.164
  161.9 0.9 fusion.168
  162.9 0.6 dynamic_slice.55
  165.4 0.9 fusion.166
  166.8 0.5 fusion.164
  167.7 0.9 fusion.168
  168.6 0.7 copy.116
  169.3 8.7 %collective-permute-done = bf16[2,512,128]{2,1,0:T(8,128)(2,1)S(1)} collective-permute-done((bf16[2,512,128]{2,1,0:T(8,128)(2,1)}, bf16[2,512,128]{2,1,0:T(8,128)(2,1)S(1)}, u32[]{:S(2)}, u32[]{:S(2)}) %collective-permute-start) | collective-permute-done | bytes 262176 | tf_op jit(solution)/shard_map/while/body/eval_jaxpr/ppermute | solution.py:30
  178.0 11.4 %while.103 = (s32[]{:T(128)}, f32[2,256,8]{1,2,0:T(8,128)S(1)}, f32[2,256,8]{1,2,0:T(8,128)S(1)}, f32[2,256,8,128]{3,1,2,0:T(8,128)S(1)}, s32[]{:T(128)}, /*inde...) while((s32[]{:T(128)}, f32[2,256,8]{1,2,0:T(8,128)S(1)}, ...), condition=%wide.region_13.13_spmd.clone, body=%wide.region_8.12_spmd.clone.sunk | while | flops 551699200 | bytes 23059792 | solution.py:132
  178.0 0.6 dynamic_slice.55
  180.5 0.9 fusion.166
  181.9 0.5 fusion.164
  182.8 0.9 fusion.168
  183.7 0.6 dynamic_slice.55
  186.2 0.9 fusion.166
  187.6 0.5 fusion.164
  188.5 0.9 fusion.168
  189.4 0.7 copy.116
  190.2 1.0 divide_convert_fusion
  191.1 0.7 copy.48
  191.8 16.8 %convolution_convert_fusion = bf16[512,8192]{1,0:T(8,128)(2,1)} fusion(bf16[1024,8192]{1,0:T(8,128)(2,1)} %param.42, bf16[64,8,8,128]{3,2,1,0:T(8,128)(2,1)S(1)} %bitcast.277), kind=kOutput, calls=%fused_computation.137 | convolution fusion | flops 8594128896 | bytes 26214400 | tf_op jit(solution)/shard_map/dot_general | solution.py:156
  208.7 0.6 log_add_fusion
  209.3 68.1 %reduce-scatter.2.cloned.1.call-done = bf16[512,1024]{1,0:T(8,128)(2,1)} async-done(((bf16[512,8192]{1,0:T(8,128)(2,1)}), bf16[512,1024]{1,0:T(8,128)(2,1)}) %reduce-scatter.2.cloned.1.call-update) | async-done | bytes 1048592 | tf_op jit(solution)/shard_map/reduce_scatter | solution.py:157
  (126 shorter events, 18.3 us)
Async XLA Ops:
  7.2 83.9 %copy-start = (bf16[8192,128]{1,0:T(8,128)(2,1)S(1)}, bf16[8192,128]{1,0:T(8,128)(2,1)}, u32[]{:S(2)}) copy-start(bf16[8192,128]{1,0:T(8,128)(2,1)} %param.40) | copy-start | bytes 6291460
  7.2 59.7 %all-gather.2.cloned.1.call-start = ((), (), s32[]{:S(2)}) async-start(), calls=%async_computation.1 | async-start | bytes 9437184 | tf_op jit(solution)/shard_map/all_gather | solution.py:61
  7.9 269.5 %reduce-scatter.2.cloned.1.call-start = ((), (), s32[]{:S(2)}) async-start(), calls=%async_computation.2 | async-start | bytes 9437184 | tf_op jit(solution)/shard_map/reduce_scatter | solution.py:157
  11.1 60.9 %copy-start.5 = (f32[8192]{0:T(1024)S(1)}, f32[8192]{0:T(1024)}, u32[]{:S(2)}) copy-start(f32[8192]{0:T(1024)} %param.38) | copy-start | bytes 98308
  96.8 1.6 copy-start.2
  112.2 0.9 copy-start.4
  113.2 1.6 copy-start.3
  119.1 1.6 copy-start.3
  124.9 10.5 %collective-permute-start = (bf16[2,512,128]{2,1,0:T(8,128)(2,1)}, bf16[2,512,128]{2,1,0:T(8,128)(2,1)S(1)}, u32[]{:S(2)}, u32[]{:S(2)}) collective-permute-start(bf16[2,512,128]{2,1,0:T(8,128)(2,1)} %get-tuple-element.2101), channel_id=1, source_target_pairs={{24,0},{0,8},{8,16},{16,24},{25,1},{1,9},{9,17},{17,25},{26,2},{2,... | collective-permute-start | bytes 786440 | tf_op jit(solution)/shard_map/while/body/eval_jaxpr/ppermute | solution.py:30
  147.6 9.6 %collective-permute-start = (bf16[2,512,128]{2,1,0:T(8,128)(2,1)}, bf16[2,512,128]{2,1,0:T(8,128)(2,1)S(1)}, u32[]{:S(2)}, u32[]{:S(2)}) collective-permute-start(bf16[2,512,128]{2,1,0:T(8,128)(2,1)} %get-tuple-element.2101), channel_id=1, source_target_pairs={{24,0},{0,8},{8,16},{16,24},{25,1},{1,9},{9,17},{17,25},{26,2},{2,... | collective-permute-start | bytes 786440 | tf_op jit(solution)/shard_map/while/body/eval_jaxpr/ppermute | solution.py:30
  169.3 8.7 %collective-permute-start = (bf16[2,512,128]{2,1,0:T(8,128)(2,1)}, bf16[2,512,128]{2,1,0:T(8,128)(2,1)S(1)}, u32[]{:S(2)}, u32[]{:S(2)}) collective-permute-start(bf16[2,512,128]{2,1,0:T(8,128)(2,1)} %get-tuple-element.2101), channel_id=1, source_target_pairs={{24,0},{0,8},{8,16},{16,24},{25,1},{1,9},{9,17},{17,25},{26,2},{2,... | collective-permute-start | bytes 786440 | tf_op jit(solution)/shard_map/while/body/eval_jaxpr/ppermute | solution.py:30
  208.7 68.7 %copy-start.1 = (bf16[8192,128]{1,0:T(8,128)(2,1)S(1)}, bf16[8192,128]{1,0:T(8,128)(2,1)}, u32[]{:S(2)}) copy-start(bf16[8192,128]{1,0:T(8,128)(2,1)} %param.40) | copy-start | bytes 6291460
Sparse Core Ops, SparseCore 0:
  9.9 56.9 all-gather.1
  208.8 68.5 reduce-scatter.1
where the time goes:
time: 285 us; the launch traced here: 284 us
  waiting for transfers between devices  152 us (53%)
  matrix products  66.3 us (23%)
  other arithmetic  26.9 us (9%)
  local copies, waits for them, and re-layouts  15.8 us (6%)
  between operations  15.4 us (5%)
  loops' own time  6.3 us (2%)
    reduce_scatter x1, waiting for transfers between devices, shards(): lax.psum_scatter(partial_terms.astype(jnp.bfloat16), 'tp', scatter_dimens...  68.1 us
    all_gather x1, waiting for transfers between devices, shards(): gathered = lax.all_gather(checkpoint, 'tp', axis=1, tiled=True)  55.8 us
    ppermute x3, waiting for transfers between devices, from_behind(): return lax.ppermute(block, axis, route)  27.3 us
    dot_general x1, matrix products, shards(): jnp.dot(attended, output_weight, preferred_element_type=jnp.float32)  16.8 us
    dot_general x1, matrix products, shards(): jnp.dot(normed, query_weight, preferred_element_type=jnp.float32)  15.5 us
    dot_general x16, matrix products, absorb(): jnp.einsum('qhk,kd->qhd', weights.astype(jnp.bfloat16), value_rows, prefe...  14.3 us
    reduce_sum x16, other arithmetic, absorb(): new_total = totals[query_slot] * shrink + jnp.sum(weights, axis=-1)  8.28 us
    dot_general x16, matrix products, absorb(): jnp.einsum('qhd,kd->qhk', query_rows, key_rows, preferred_element_type=jn...  7.43 us
  transfers between devices with their start and end apart: 5, of which 5 were waited for; matrix products, arithmetic and copies ran while one was open for 1% of the time, Pallas kernels for 0%

commit v1 on v0

--- a/solution.py
+++ b/solution.py
@@ -1,9 +1,13 @@
+import functools
 import math
 
 import jax
 import jax.numpy as jnp
 from jax import lax
+from jax.experimental import pallas as pl
+from jax.experimental.pallas import tpu as pltpu
 from jax.sharding import PartitionSpec as P
+
 
 KV_HEADS = 8
 HEAD_DIM = 128
@@ -12,6 +16,471 @@
 rope_base = 500000.0
 norm_epsilon = 1e-05
 masked_score = -1e30
+f32 = jnp.float32
+bf16 = jnp.bfloat16
+VMEM = 50 * 2**20
+
+
+def flip(block, axis, mask):
+    count = lax.axis_size(axis)
+    return lax.ppermute(block, axis, [(i, i ^ mask) for i in range(count)])
+
+
+def from_behind(block, axis, distance):
+    devices = range(lax.axis_size(axis))
+    route = [((i - distance) % len(devices), i) for i in devices]
+    return lax.ppermute(block, axis, route)
+
+
+def rope_tables(positions):
+    lane = jnp.arange(HEAD_DIM, dtype=jnp.int32)
+    pair_index = (lane // 2).astype(f32)
+    inverse_rates = rope_base ** (-2.0 * pair_index / HEAD_DIM)
+    angles = positions.astype(f32)[:, None] * inverse_rates[None, :]
+    sine = jnp.sin(angles)
+    return jnp.cos(angles), jnp.where(lane % 2 == 0, -sine, sine)
+
+
+def normalise(rank, gains, first, pieces, weights, carry=None, tables=None):
+    count = len(pieces)
+    rows = sum(r for _, _, r in pieces[0])
+    width = pieces[0][0][0].shape[1]
+    flat = [part for piece in pieces for part, _, _ in piece]
+    most = max(len(piece) for piece in pieces)
+    total_width = gains.shape[0] * width
+    columns = sum(w.shape[1] for w, _ in weights)
+    n = len(weights)
+    given = list(carry or []) + list(tables or [])
+    ahead = min(count, 3)
+
+    def body(rank_ref, gain_ref, *refs):
+        piece_refs, refs = refs[: len(flat)], refs[len(flat) :]
+        weight_refs, refs = refs[:n], refs[n:]
+        given_refs, refs = refs[: len(given)], refs[len(given) :]
+        scaled, product, *others = refs[: 4 if tables else 3]
+        taken, held, total, squares, taken_sems, held_sems = refs[4 if tables else 3 :]
+
+        def fetch(j):
+            at = sum(len(piece) for piece in pieces[:j])
+            row = 0
+            for p, (_, start, size) in enumerate(pieces[j]):
+                source = piece_refs[at + p].at[pl.ds(start, size)]
+                yield pltpu.make_async_copy(source, taken.at[j, pl.ds(row, size)], taken_sems.at[j, p])
+                row += size
+            start = pl.multiple_of((rank_ref[0] ^ (first + j)) * width, width)
+            column = 0
+            for i, (w, _) in enumerate(weights):
+                size = w.shape[1]
+                target = held.at[j, :, pl.ds(column, size)]
+                yield pltpu.make_async_copy(weight_refs[i].at[pl.ds(start, width)], target, held_sems.at[i, j])
+                column += size
+
+        def begin(j):
+            for copy in fetch(j):
+                copy.start()
+
+        for j in range(ahead):
+            begin(j)
+        if carry:
+            total[...] = given_refs[0][...]
+            squares[...] = given_refs[1][...]
+        else:
+            total[...] = jnp.zeros_like(total)
+            squares[...] = jnp.zeros_like(squares)
+
+        def step(j, _):
+            for m in range(count):
+
+                @pl.when(j == m)
+                def _(m=m):
+                    if m + ahead < count:
+                        begin(m + ahead)
+                    for copy in fetch(m):
+                        copy.wait()
+
+            gain = gain_ref[rank_ref[0] ^ (first + j)]
+            for r in range(0, rows, 32):
+                x = taken[j, r : r + 32].astype(f32)
+                scaled[j, r : r + 32] = (x * gain).astype(bf16)
+                square = x * x
+                part = square[:, :128]
+                for c in range(128, width, 128):
+                    part = part + square[:, c : c + 128]
+                squares[r : r + 32] += part
+            total[...] += jnp.dot(scaled[j], held[j], preferred_element_type=f32)
+            return 0
+
+        lax.fori_loop(0, count, step, 0)
+        if not tables:
+            product[...] = total[...]
+            others[0][...] = squares[...]
+            return
+        mean = jnp.sum(squares[...], axis=1, keepdims=True) / total_width
+        r = lax.rsqrt(mean + norm_epsilon)
+        cos_ref, sin_ref = given_refs[-2:]
+        cr, sr = cos_ref[...] * r, sin_ref[...] * r
+        others[0][...] = cr
+        others[1][...] = sr
+        column = 0
+        for w, rotated in weights:
+            for c in range(column, column + w.shape[1], HEAD_DIM):
+                a = total[:, c : c + HEAD_DIM]
+                a = turn(a, cr, sr) if rotated else a * r
+                product[:, c : c + HEAD_DIM] = a.astype(bf16)
+            column += w.shape[1]
+
+    whole = lambda shape: pl.BlockSpec(shape, lambda i, t: (0,) * len(shape))
+    far = pl.BlockSpec(memory_space=pltpu.MemorySpace.HBM)
+    out_shape = [jax.ShapeDtypeStruct((count, rows, width), bf16)]
+    if tables:
+        out_shape += [jax.ShapeDtypeStruct((rows, columns), bf16)] + [jax.ShapeDtypeStruct((rows, HEAD_DIM), f32)] * 2
+    else:
+        out_shape += [jax.ShapeDtypeStruct((rows, c), f32) for c in (columns, 128)]
+    grid_spec = pltpu.PrefetchScalarGridSpec(
+        num_scalar_prefetch=1,
+        grid=(1,),
+        in_specs=[whole(gains.shape)] + [far] * (len(flat) + n) + [whole(g.shape) for g in given],
+        out_specs=[whole(o.shape) for o in out_shape],
+        scratch_shapes=[
+            pltpu.VMEM((count, rows, width), bf16),
+            pltpu.VMEM((count, width, columns), bf16),
+            pltpu.VMEM((rows, columns), f32),
+            pltpu.VMEM((rows, 128), f32),
+            pltpu.SemaphoreType.DMA((count, most)),
+            pltpu.SemaphoreType.DMA((n, count)),
+        ],
+    )
+    return pl.pallas_call(
+        body,
+        grid_spec=grid_spec,
+        out_shape=out_shape,
+        compiler_params=pltpu.CompilerParams(vmem_limit_bytes=VMEM),
+        cost_estimate=pl.CostEstimate(
+            flops=2 * rows * count * width * columns,
+            bytes_accessed=2 * count * width * (rows + columns),
+            transcendentals=0,
+        ),
+        name="normalise",
+    )(rank, gains, *flat, *[w for w, _ in weights], *given)
+
+
+def turn(a, cosine, sine):
+    even = lax.broadcasted_iota(jnp.int32, a.shape, 1) % 2 == 0
+    other = jnp.where(even, pltpu.roll(a, HEAD_DIM - 1, 1), pltpu.roll(a, 1, 1))
+    return a * cosine + other * sine
+
+
+def project(rank, chunks, weight):
+    rows, width = chunks[0][0][0].shape[1:]
+    sizes = [s.shape[0] for s in chunks[0][0]]
+    count = sum(sizes)
+    columns = weight.shape[1]
+    ahead = 4
+    n = len(chunks)
+
+    def body(rank_ref, *refs):
+        table_refs, refs = refs[: 2 * n], refs[2 * n :]
+        scaled_refs, refs = refs[: n * len(sizes)], refs[n * len(sizes) :]
+        weight_ref, *outs = refs[: 1 + n]
+        held, total, sems = refs[1 + n :]
+
+        def fetch(j):
+            start = pl.multiple_of((rank_ref[0] ^ j) * width, width)
+            slot = j % ahead
+            return pltpu.make_async_copy(weight_ref.at[pl.ds(start, width)], held.at[slot], sems.at[slot])
+
+        for j in range(ahead - 1):
+            fetch(j).start()
+        total[...] = jnp.zeros_like(total)
+        first = 0
+        for i, size in enumerate(sizes):
+
+            def step(j, _, i=i, first=first):
+                @pl.when(j + ahead - 1 < count)
+                def _():
+                    fetch(j + ahead - 1).start()
+
+                fetch(j).wait()
+                for c in range(n):
+                    lhs = scaled_refs[c * len(sizes) + i][j - first]
+                    total[c] += jnp.dot(lhs, held[j % ahead], preferred_element_type=f32)
+                return 0
+
+            lax.fori_loop(first, first + size, step, 0)
+            first += size
+        for i in range(n):
+            for c in range(0, columns, HEAD_DIM):
+                a = turn(total[i, :, c : c + HEAD_DIM], table_refs[2 * i][...], table_refs[2 * i + 1][...])
+                outs[i][:, c : c + HEAD_DIM] = a.astype(bf16)
+
+    tables = [t for _, *pair in chunks for t in pair]
+    scaled = [s for pieces, _, _ in chunks for s in pieces]
+    whole = lambda shape: pl.BlockSpec(shape, lambda i, t: (0,) * len(shape))
+    grid_spec = pltpu.PrefetchScalarGridSpec(
+        num_scalar_prefetch=1,
+        grid=(1,),
+        in_specs=[whole(t.shape) for t in tables]
+        + [whole(s.shape) for s in scaled]
+        + [pl.BlockSpec(memory_space=pltpu.MemorySpace.HBM)],
+        out_specs=[whole((rows, columns))] * n,
+        scratch_shapes=[
+            pltpu.VMEM((ahead, width, columns), bf16),
+            pltpu.VMEM((n, rows, columns), f32),
+            pltpu.SemaphoreType.DMA((ahead,)),
+        ],
+    )
+    return pl.pallas_call(
+        body,
+        grid_spec=grid_spec,
+        out_shape=[jax.ShapeDtypeStruct((rows, columns), bf16)] * n,
+        compiler_params=pltpu.CompilerParams(vmem_limit_bytes=VMEM),
+        cost_estimate=pl.CostEstimate(
+            flops=2 * n * rows * count * width * columns, bytes_accessed=2 * count * width * columns, transcendentals=0
+        ),
+        name="project",
+    )(rank, *tables, *scaled, weight)
+
+
+def attend(queries, slot, block_order, context_rank, pieces):
+    rows = queries.shape[0]
+    heads = queries.shape[1] // HEAD_DIM
+    key_rows = pieces[0].shape[0]
+    tile = min(rows, key_rows, 256)
+    q_tiles, k_tiles = rows // tile, key_rows // tile
+    factor = math.log2(math.e) / math.sqrt(HEAD_DIM)
+    n = len(pieces)
+    sources = n // 2
+
+    def body(order_ref, place_ref, q_ref, *refs):
+        piece_refs = refs[:n]
+        outs = refs[n:-5]
+        keys, values, top, total, acc = refs[-5:]
+        step = pl.program_id(0)
+
+        @pl.when(step == 0)
+        def _():
+            top[...] = jnp.full_like(top, masked_score)
+            total[...] = jnp.zeros_like(total)
+            acc[...] = jnp.zeros_like(acc)
+
+        for j in range(n):
+
+            @pl.when(step == j)
+            def _(j=j):
+                keys[...] = piece_refs[j][:, :HEAD_DIM]
+                values[...] = piece_refs[j][:, HEAD_DIM:].T
+
+        ahead = lax.broadcasted_iota(jnp.int32, (tile, tile), 0) - lax.broadcasted_iota(jnp.int32, (tile, tile), 1)
+        for ki in range(k_tiles):
+            source = (place_ref[0] - step // 2 + sources) % sources
+            k0 = order_ref[2 * source + step % 2] * key_rows + ki * tile
+            for qi in range(q_tiles):
+                q0 = order_ref[2 * place_ref[0] + slot] * rows + qi * tile
+                span = slice(qi * tile, (qi + 1) * tile)
+
+                @pl.when(k0 <= q0 + tile - 1)
+                def _(ki=ki, k0=k0, q0=q0, span=span):
+                    k = keys[ki * tile : (ki + 1) * tile]
+                    v = values[:, ki * tile : (ki + 1) * tile]
+
+                    held = []
+                    for h in range(heads):
+                        q = q_ref[span, h * HEAD_DIM : (h + 1) * HEAD_DIM]
+                        s = lax.dot_general(k, q, (((1,), (1,)), ((), ())), preferred_element_type=f32)
+                        held.append(jnp.where(ahead <= q0 - k0, s * factor, masked_score))
+                    for h in range(heads):
+                        old = top[h, :, span]
+                        new = jnp.maximum(old, jnp.max(held[h], axis=0, keepdims=True))
+                        p = jnp.exp2(held[h] - new)
+                        shrink = jnp.exp2(old - new)
+                        top[h, :, span] = new
+                        total[h, :, span] = total[h, :, span] * shrink + jnp.sum(p, axis=0, keepdims=True)
+                        held[h] = (p.astype(bf16), shrink)
+                    for h in range(heads):
+                        p, shrink = held[h]
+                        acc[h, :, span] = acc[h, :, span] * shrink + jnp.dot(v, p, preferred_element_type=f32)
+
+        @pl.when(step == n - 1)
+        def _():
+            for h in range(heads):
+                t = total[h]
+                outs[1][h] = (top[h] + jnp.log2(t)) * math.log(2.0)
+                outs[0][:, h * HEAD_DIM : (h + 1) * HEAD_DIM] = (acc[h] / t).T.astype(bf16)
+
+    small = (heads, 1, rows)
+    big = (heads, HEAD_DIM, rows)
+    whole = lambda shape: pl.BlockSpec(shape, lambda i, a, b: (0,) * len(shape))
+    out_shape = [jax.ShapeDtypeStruct(queries.shape, bf16), jax.ShapeDtypeStruct(small, f32)]
+    grid_spec = pltpu.PrefetchScalarGridSpec(
+        num_scalar_prefetch=2,
+        grid=(n,),
+        in_specs=[whole(queries.shape)] + [whole(p.shape) for p in pieces],
+        out_specs=[whole(o.shape) for o in out_shape],
+        scratch_shapes=[
+            pltpu.VMEM((key_rows, HEAD_DIM), bf16),
+            pltpu.VMEM((HEAD_DIM, key_rows), bf16),
+            pltpu.VMEM(small, f32),
+            pltpu.VMEM(small, f32),
+            pltpu.VMEM(big, f32),
+        ],
+    )
+    return pl.pallas_call(
+        body,
+        grid_spec=grid_spec,
+        out_shape=out_shape,
+        compiler_params=pltpu.CompilerParams(vmem_limit_bytes=VMEM),
+        cost_estimate=pl.CostEstimate(
+            flops=4 * rows * heads * n * key_rows * HEAD_DIM,
+            bytes_accessed=2 * rows * heads * HEAD_DIM,
+            transcendentals=rows * heads * n * key_rows,
+        ),
+        name="attend",
+    )(block_order, context_rank, queries, *pieces)
+
+
+def spread(rank, slots, own, other, own_weight, other_weight):
+    rows, inner = own.shape
+    half = rows // 2
+    width = other_weight[0].shape[1]
+    n = len(slots)
+    cuts = 2
+    deep = inner // cuts
+
+    def body(rank_ref, a_ref, b_ref, w_ref, *refs):
+        other_refs, refs = refs[:n], refs[n:]
+        outs, (held, sems) = refs[: 2 * n], refs[2 * n :]
+
+        def hold(j, side, c):
+            start = pl.multiple_of((rank_ref[0] ^ (2 * slots[j])) * width, width)
+            depth = pl.ds(c * deep, deep)
+            source = other_refs[j].at[depth] if side else w_ref.at[depth, pl.ds(start, width)]
+            return pltpu.make_async_copy(source, held.at[j, side, depth], sems.at[j, side, c])
+
+        order = [(j, side, c) for j in range(n) for side in range(2) for c in range(cuts)]
+        ahead = 3
+        for key in order[:ahead]:
+            hold(*key).start()
+        for j in range(n):
+            full = None
+            for side, ref in enumerate((a_ref, b_ref)):
+                for c in range(cuts):
+                    at = order.index((j, side, c)) + ahead
+                    if at < len(order):
+                        hold(*order[at]).start()
+                    hold(j, side, c).wait()
+                    cut = slice(c * deep, (c + 1) * deep)
+                    term = jnp.dot(ref[:, cut], held[j, side, cut], preferred_element_type=f32)
+                    full = term if full is None else full + term
+            outs[2 * j][...] = full[:half].astype(bf16)
+            outs[2 * j + 1][...] = full[half:].astype(bf16)
+
+    whole = lambda shape: pl.BlockSpec(shape, lambda i, t: (0,) * len(shape))
+    far = pl.BlockSpec(memory_space=pltpu.MemorySpace.HBM)
+    grid_spec = pltpu.PrefetchScalarGridSpec(
+        num_scalar_prefetch=1,
+        grid=(1,),
+        in_specs=[whole(own.shape), whole(other.shape)] + [far] * (1 + n),
+        out_specs=[whole((half, width))] * (2 * n),
+        scratch_shapes=[pltpu.VMEM((n, 2, inner, width), bf16), pltpu.SemaphoreType.DMA((n, 2, cuts))],
+    )
+    return pl.pallas_call(
+        body,
+        grid_spec=grid_spec,
+        out_shape=[jax.ShapeDtypeStruct((half, width), bf16)] * (2 * n),
+        compiler_params=pltpu.CompilerParams(vmem_limit_bytes=VMEM),
+        cost_estimate=pl.CostEstimate(
+            flops=4 * rows * inner * width * n, bytes_accessed=4 * inner * width * n, transcendentals=0
+        ),
+        name="spread",
+    )(rank, own, other, own_weight, *other_weight)
+
+
+def after(value, *others):
+    return lax.optimization_barrier((value, *others))[0]
+
+
+def plane_shards(checkpoint, norm_gain, query_weight, key_weight, value_weight, output_weight, block_order):
+    tok_rows, width = checkpoint.shape
+    block_rows = tok_rows // 2
+    context_rank = lax.axis_index("cp")
+    context_size = lax.axis_size("cp")
+    tensor_rank = lax.axis_index("tp")
+    rank = tensor_rank.astype(jnp.int32)[None]
+    row_offsets = jnp.arange(block_rows, dtype=jnp.int32)
+    own_blocks = lax.dynamic_slice_in_dim(block_order, 2 * context_rank, 2)
+    positions = (own_blocks[:, None] * block_rows + row_offsets[None, :]).reshape(tok_rows)
+    gains = norm_gain.reshape(-1, 1, width)
+    CORE, X, Y = 1, 2, 4
+
+    def tp(block, mask):
+        return flip(block, "tp", mask)
+
+    half = block_rows // 2
+    own_core = tp(checkpoint, CORE)
+
+    gathered = []
+    for n in range(2):
+        start = n * block_rows
+        if n:
+            checkpoint_later = after(checkpoint, gathered[0][4][0][0])
+        else:
+            checkpoint_later = checkpoint
+        lo = checkpoint_later[start : start + half]
+        hi = checkpoint_later[start + half : start + block_rows]
+        x_hi, y_lo = tp(hi, X), tp(lo, Y)
+        x_lo, y_hi = tp(lo, X), tp(hi, Y)
+        d_lo, d_hi = tp(y_lo, X), tp(x_hi, Y)
+        pieces = [[(checkpoint, start, block_rows)], [(own_core, start, block_rows)]]
+        for part in ((x_lo, x_hi), (y_lo, y_hi), (d_lo, d_hi)):
+            pieces.append([(p, 0, half) for p in part])
+            pieces.append([(tp(p, CORE), 0, half) for p in part])
+        gathered.append(pieces)
+
+    later = output_weight
+    other_weight = []
+    for slot in range(lax.axis_size("tp") // 2):
+        column = ((tensor_rank ^ CORE) ^ (2 * slot)) * width
+        other_weight.append(lax.dynamic_slice_in_dim(later, column, width, 1))
+    other_weight = [tp(w, CORE) for w in other_weight]
+
+    cosine, sine = rope_tables(positions)
+    tables = [(cosine[n * block_rows : (n + 1) * block_rows], sine[n * block_rows : (n + 1) * block_rows]) for n in range(2)]
+    key_value = [(key_weight, True), (value_weight, False)]
+    early = 6
+
+    chunks, context = [], []
+    for n in range(2):
+        scaled, *sums = normalise(rank, gains, 0, gathered[n][:early], key_value)
+        rest, own, cosine, sine = normalise(rank, gains, early, gathered[n][early:], key_value, sums, tables[n])
+        others = []
+        for d in range(1, context_size):
+            others.append(from_behind(own, "cp", d))
+        context.append([own, *others])
+        chunks.append(([scaled, rest], cosine, sine))
+    queries = project(rank, chunks, query_weight)
+
+    place = context_rank.astype(jnp.int32)[None]
+    pieces = [piece for pair in zip(*context) for piece in pair]
+    results, normalizers = [], []
+    for c in range(2):
+        attended, normalizer = attend(queries[c], c, block_order, place, pieces)
+        normalizers.append(normalizer[:, 0])
+        partner = tp(attended, CORE)
+
+        def deliver(slots):
+            return spread(rank, slots, attended, partner, output_weight, [other_weight[s] for s in slots])
+
+        d_lo, d_hi = deliver([3])
+        d_lo, d_hi = tp(d_lo, X), tp(d_hi, Y)
+        x_lo, x_hi, y_lo, y_hi = deliver([1, 2])
+        s_lo, s_hi = deliver([0])
+        add = lambda *terms: functools.reduce(jnp.add, [t.astype(f32) for t in terms])
+        x_lo, y_hi = tp(x_lo, X), tp(y_hi, Y)
+        x_hi = tp(add(x_hi, d_hi).astype(bf16), X)
+        y_lo = tp(add(y_lo, d_lo).astype(bf16), Y)
+        results.append(add(s_lo, x_lo, y_lo).astype(bf16))
+        results.append(add(s_hi, x_hi, y_hi).astype(bf16))
+    return jnp.concatenate(results, axis=0), jnp.concatenate(normalizers, axis=1)
 
 
 def partner_2(block, axis, stride):
@@ -21,12 +490,6 @@
         high = low | 1 << stride
         if high != low and high < count:
             route += [(low, high), (high, low)]
-    return lax.ppermute(block, axis, route)
-
-
-def from_behind(block, axis, distance):
-    devices = range(lax.axis_size(axis))
-    route = [((i - distance) % len(devices), i) for i in devices]
     return lax.ppermute(block, axis, route)
 
 
@@ -145,7 +608,7 @@
         source = (context_rank - turn_index) % context_size
         return (visit_rows(current, travelling, source * tok_rows), travelling)
 
-    running, unused = lax.fori_loop(1, context_size, pass_turn, (running, key_value))
+    running, _ = lax.fori_loop(1, context_size, pass_turn, (running, key_value))
     top_scores, totals, weighted = running
     attended = (
         (weighted / totals[..., None])
@@ -161,8 +624,13 @@
 
 
 def solution(mesh):
+    plane = mesh.shape["tp"] == KV_HEADS
+
+    def body(*args):
+        return plane_shards(*args)
+
     return jax.shard_map(
-        shards,
+        body if plane else shards,
         mesh=mesh,
         in_specs=(
             P("cp", "tp"),

time: 285 us -> 169 us (0.59)
  waiting for transfers between devices: 152 us -> 42.9 us
  matrix products: 66.3 us -> 0 us
  Pallas kernels: 0 us -> 64 us
  starting transfers between devices: 1.62 us -> 43 us
  other arithmetic: 26.9 us -> 3.57 us
  between operations: 15.4 us -> 1.1 us
  loops' own time: 6.3 us -> 0 us
  local copies, waits for them, and re-layouts: 15.8 us -> 11.7 us
    reduce_scatter x1 -> x0, waiting for transfers between devices: 68.1 us -> none  [shards(): lax.psum_scatter(partial_terms.astype(jnp.bfloat16), 'tp', scatter_dimens...]
    dot_general x36 -> x0, matrix products: 66.3 us -> none  [the longest x1 16.8 us: shards(): jnp.dot(attended, output_weight, preferred_element_type=jnp.float32)]
    pallas_call x0 -> x13, Pallas kernels: none -> 64 us  [the longest x6 21 us: spread(): pl.pallas_call(body, grid_spec=grid_spec, out_shape=[jax.ShapeDtypeStruct...]
    all_gather x1 -> x0, waiting for transfers between devices: 55.8 us -> none  [shards(): gathered = lax.all_gather(checkpoint, 'tp', axis=1, tiled=True)]
    ppermute x0 -> x43, starting transfers between devices: none -> 34.2 us  [flip(): return lax.ppermute(block, axis, [(i, i ^ mask) for i in range(count)])]
    ppermute x0 -> x43, waiting for transfers between devices: none -> 34.1 us  [flip(): return lax.ppermute(block, axis, [(i, i ^ mask) for i in range(count)])]
    ppermute x3 -> x6, waiting for transfers between devices: 27.3 us -> 8.86 us  [from_behind(): return lax.ppermute(block, axis, route)]
    reduce_sum x17 -> x0, other arithmetic: 13.4 us -> none  [the longest x16 8.28 us: absorb(): new_total = totals[query_slot] * shrink + jnp.sum(weights, axis=-1)]
  transfers between devices with their start and end apart: 5 -> 49, of which waited for: 5 -> 13; matrix products, arithmetic and copies ran while one was open for 1% -> 7% of each run, Pallas kernels for 0% -> 38%
where the time goes in v1:
time: 169 us; the launch traced here: 166 us
  Pallas kernels  64 us (38%)
  starting transfers between devices  43 us (25%)
  waiting for transfers between devices  42.9 us (25%)
  local copies, waits for them, and re-layouts  11.7 us (7%)
  other arithmetic  3.57 us (2%)
    ppermute x43, starting transfers between devices, flip(): return lax.ppermute(block, axis, [(i, i ^ mask) for i in range(count)])  34.2 us
    ppermute x43, waiting for transfers between devices, flip(): return lax.ppermute(block, axis, [(i, i ^ mask) for i in range(count)])  34.1 us
    pallas_call x6, Pallas kernels, spread(): pl.pallas_call(body, grid_spec=grid_spec, out_shape=[jax.ShapeDtypeStruct...  21 us
    pallas_call x1, Pallas kernels, project(): pl.pallas_call(body, grid_spec=grid_spec, out_shape=[jax.ShapeDtypeStruct...  16 us
    pallas_call x4, Pallas kernels, normalise(): pl.pallas_call(body, grid_spec=grid_spec, out_shape=out_shape, compiler_p...  14.5 us
    pallas_call x2, Pallas kernels, attend(): pl.pallas_call(body, grid_spec=grid_spec, out_shape=out_shape, compiler_p...  12.5 us
    ppermute x6, waiting for transfers between devices, from_behind(): return lax.ppermute(block, axis, route)  8.86 us
    ppermute x6, starting transfers between devices, from_behind(): return lax.ppermute(block, axis, route)  8.83 us
  transfers between devices with their start and end apart: 49, of which 13 were waited for; matrix products, arithmetic and copies ran while one was open for 7% of the time, Pallas kernels for 38%

profile of v1, /device:TPU:0, one launch (start us, length us, event | category | flops | bytes accessed | tf_op | source)
XLA Modules:
  0.0 166.3 jit_solution(2957898421762949396)
XLA Ops:
  0.7 1.2 fusion.5
  1.8 3.1 %collective-permute-start = (bf16[128,1024]{1,0:T(8,128)(2,1)S(1)}, bf16[128,1024]{1,0:T(8,128)(2,1)S(1)}, u32[]{:S(2)}, u32[]{:S(2)}) collective-permute-start(bf16[128,1024]{1,0:T(8,128)(2,1)S(1)} %get-tuple-element.83), channel_id=1, source_target_pairs={{0,4},{1,5},{2,6},{3,7},{4,0},{5,1},{6,2},{7,3},{8,12},{9,13},{10,... | collective-permute-start | bytes 786440 | tf_op jit(solution)/shard_map/ppermute | solution.py:26
  5.0 1.9 %collective-permute-start.2 = (bf16[128,1024]{1,0:T(8,128)(2,1)S(1)}, bf16[128,1024]{1,0:T(8,128)(2,1)S(1)}, u32[]{:S(2)}, u32[]{:S(2)}) collective-permute-start(bf16[128,1024]{1,0:T(8,128)(2,1)S(1)} %get-tuple-element.82), channel_id=1, source_target_pairs={{0,2},{1,3},{2,0},{3,1},{4,6},{5,7},{6,4},{7,5},{8,10},{9,11},{10,... | collective-permute-start | bytes 786440 | tf_op jit(solution)/shard_map/ppermute | solution.py:26
  6.9 5.2 %collective-permute-done.refs_6_ = bf16[128,1024]{1,0:T(8,128)(2,1)S(1)} collective-permute-done((bf16[128,1024]{1,0:T(8,128)(2,1)S(1)}, bf16[128,1024]{1,0:T(8,128)(2,1)S(1)}, u32[]{:S(2)}, u32[]{:S(2)}) %collective-permute-start) | collective-permute-done | bytes 262176 | tf_op jit(solution)/shard_map/ppermute | solution.py:26
  12.0 1.8 %fusion.4 = (bf16[128,1024]{1,0:T(8,128)(2,1)S(1)}, bf16[128,1024]{1,0:T(8,128)(2,1)}) fusion(bf16[512,1024]{1,0:T(8,128)(2,1)} %refs_0_.3), kind=kLoop, calls=%fused_computation.30 | loop fusion | bytes 1048576 | tf_op jit(solution)/shard_map/slice | solution.py:429
  13.8 2.0 %collective-permute-start.15 = (bf16[128,1024]{1,0:T(8,128)(2,1)S(1)}, bf16[128,1024]{1,0:T(8,128)(2,1)S(1)}, u32[]{:S(2)}, u32[]{:S(2)}) collective-permute-start(bf16[128,1024]{1,0:T(8,128)(2,1)S(1)} %get-tuple-element.80), channel_id=1, source_target_pairs={{0,2},{1,3},{2,0},{3,1},{4,6},{5,7},{6,4},{7,5},{8,10},{9,11},{10,... | collective-permute-start | bytes 786440 | tf_op jit(solution)/shard_map/ppermute | solution.py:26
  15.8 1.5 collective-permute-start.22
  17.7 2.0 %collective-permute-start.19 = (bf16[128,1024]{1,0:T(8,128)(2,1)}, bf16[128,1024]{1,0:T(8,128)(2,1)S(1)}, u32[]{:S(2)}, u32[]{:S(2)}) collective-permute-start(bf16[128,1024]{1,0:T(8,128)(2,1)} %get-tuple-element.81), channel_id=1, source_target_pairs={{0,2},{1,3},{2,0},{3,1},{4,6},{5,7},{6,4},{7,5},{8,10},{9,11},{10,... | collective-permute-start | bytes 786440 | tf_op jit(solution)/shard_map/ppermute | solution.py:26
  19.7 1.5 collective-permute-start.13
  21.2 0.8 collective-permute-done.15.refs_3_
  22.0 2.8 %collective-permute-done.22.refs_7_ = bf16[128,1024]{1,0:T(8,128)(2,1)S(1)} collective-permute-done((bf16[128,1024]{1,0:T(8,128)(2,1)S(1)}, bf16[128,1024]{1,0:T(8,128)(2,1)S(1)}, u32[]{:S(2)}, u32[]{:S(2)}) %collective-permute-start.22) | collective-permute-done | bytes 262176 | tf_op jit(solution)/shard_map/ppermute | solution.py:26
  24.8 1.7 %collective-permute-start.16 = (bf16[128,1024]{1,0:T(8,128)(2,1)S(1)}, bf16[128,1024]{1,0:T(8,128)(2,1)S(1)}, u32[]{:S(2)}, u32[]{:S(2)}) collective-permute-start(bf16[128,1024]{1,0:T(8,128)(2,1)S(1)} %collective-permute-done.15.refs_3_), channel_id=1, source_target_pairs={{0,4},{1,5},{2,6},{3,7},{4,0},{5,1},{6,2},{7,3},{8,12},{9,13},{10,... | collective-permute-start | bytes 786440 | tf_op jit(solution)/shard_map/ppermute | solution.py:26
  26.5 3.9 %collective-permute-done.13.refs_6_ = bf16[128,1024]{1,0:T(8,128)(2,1)S(1)} collective-permute-done((bf16[128,1024]{1,0:T(8,128)(2,1)}, bf16[128,1024]{1,0:T(8,128)(2,1)S(1)}, u32[]{:S(2)}, u32[]{:S(2)}) %collective-permute-start.13) | collective-permute-done | bytes 262176 | tf_op jit(solution)/shard_map/ppermute | solution.py:26
  30.4 0.4 collective-permute-start.14
  31.0 0.7 copy-done.2
  31.8 0.5 collective-permute-start.20
  32.3 1.4 collective-permute-done.16.refs_1_
  33.7 3.2 %collective-permute-done.14.refs_0_ = bf16[128,1024]{1,0:T(8,128)(2,1)} collective-permute-done((bf16[128,1024]{1,0:T(8,128)(2,1)S(1)}, bf16[128,1024]{1,0:T(8,128)(2,1)}, u32[]{:S(2)}, u32[]{:S(2)}) %collective-permute-start.14) | collective-permute-done | bytes 262176 | tf_op jit(solution)/shard_map/ppermute | solution.py:26
  37.0 1.0 negate_select_fusion
  38.0 0.5 collective-permute-start.7
  38.7 1.8 %collective-permute-start.3 = (bf16[128,1024]{1,0:T(8,128)(2,1)S(1)}, bf16[128,1024]{1,0:T(8,128)(2,1)S(1)}, u32[]{:S(2)}, u32[]{:S(2)}) collective-permute-start(bf16[128,1024]{1,0:T(8,128)(2,1)S(1)} %collective-permute-done.2.refs_3_), channel_id=1, source_target_pairs={{0,4},{1,5},{2,6},{3,7},{4,0},{5,1},{6,2},{7,3},{8,12},{9,13},{10,... | collective-permute-start | bytes 786440 | tf_op jit(solution)/shard_map/ppermute | solution.py:26
  40.5 1.5 collective-permute-start.1
  42.0 0.9 copy-done.3
  43.0 5.1 %normalise.6 = (bf16[6,256,1024]{2,1,0:T(8,128)(2,1)}, f32[256,256]{1,0:T(8,128)S(1)}, f32[256,128]{1,0:T(8,128)S(1)}) custom-call(s32[1]{0:T(128)} %bitcast.rank_ref, f32[8,1,1024]{2,1,0:T(1,128)S(1)} %bitcast.12, bf16[512,1024]{1,0:T(8,128)(2,1)S(1)} %copy-done, bf16[512,1024]{1,0:T(8,128)(2,1)} %collective-permute-done.6.refs_1_, ...), custom_call_target="tpu_custom_call" | custom-call | flops 805306368 | bytes 6291456 | tf_op jit(solution)/shard_map/normalise/pallas_call | solution.py:153
  48.0 2.2 %normalise.7 = (bf16[2,256,1024]{2,1,0:T(8,128)(2,1)S(1)}, bf16[256,256]{1,0:T(8,128)(2,1)S(1)}, f32[256,128]{1,0:T(8,128)S(1)}, f32[256,128]{1,0:T(8,128)S(1)}) custom-call(s32[1]{0:T(128)} %bitcast.rank_ref, f32[8,1,1024]{2,1,0:T(1,128)S(1)} %bitcast.13, bf16[128,1024]{1,0:T(8,128)(2,1)} %collective-permute-done.14.refs_0_, ...), custom_call_target="tpu_custom_call" | custom-call | flops 268435456 | bytes 2097152 | tf_op jit(solution)/shard_map/normalise/pallas_call | solution.py:153
  50.3 0.6 collective-permute-start.11
  50.9 0.4 collective-permute-start.5
  51.4 1.2 collective-permute-done.1.refs_0_
  52.6 3.8 %collective-permute-start.30 = (bf16[256,256]{1,0:T(8,128)(2,1)S(1)}, bf16[256,256]{1,0:T(8,128)(2,1)S(1)}, u32[]{:S(2)}, u32[]{:S(2)}) collective-permute-start(bf16[256,256]{1,0:T(8,128)(2,1)S(1)} %get-tuple-element.54.refs_1_), channel_id=1, source_target_pairs={{8,0},{16,8},{24,16},{0,24},{9,1},{17,9},{25,17},{1,25},{10,2},{18... | collective-permute-start | bytes 393224 | tf_op jit(solution)/shard_map/ppermute | solution.py:32
  56.3 7.0 %constant_dynamic-slice_fusion.3 = (bf16[1024,1024]{1,0:T(8,128)(2,1)}, bf16[1024,1024]{1,0:T(8,128)(2,1)}, bf16[1024,1024]{1,0:T(8,128)(2,1)}, bf16[1024,1024]{1,0:T(8,128)(2,1)}) fusion(bf16[1024,8192]{1,0:T(8,128)(2,1)} %w_ref.11, s32[]{:T(128)S(6)} %select_n.39, s32[]{:T(128)S(6)} %select_n.42, s32[]{:T(128)S(6)} %select_n.41, s32[]{:T(128)S(6)} %select_n.40), kind=kLoop, calls=%fused_computation.24 | loop fusion | bytes 16777232 | tf_op jit(solution)/shard_map/dynamic_slice | solution.py:443
  63.6 5.1 %normalise.4 = (bf16[6,256,1024]{2,1,0:T(8,128)(2,1)}, f32[256,256]{1,0:T(8,128)S(1)}, f32[256,128]{1,0:T(8,128)S(1)}) custom-call(s32[1]{0:T(128)} %bitcast.rank_ref, f32[8,1,1024]{2,1,0:T(1,128)S(1)} %bitcast.14, bf16[512,1024]{1,0:T(8,128)(2,1)S(1)} %copy-done, bf16[512,1024]{1,0:T(8,128)(2,1)} %collective-permute-done.6.refs_1_, ...), custom_call_target="tpu_custom_call" | custom-call | flops 805306368 | bytes 6291456 | tf_op jit(solution)/shard_map/normalise/pallas_call | solution.py:153
  68.7 1.1 collective-permute-start.26
  69.8 2.1 %normalise.5 = (bf16[2,256,1024]{2,1,0:T(8,128)(2,1)S(1)}, bf16[256,256]{1,0:T(8,128)(2,1)S(1)}, f32[256,128]{1,0:T(8,128)S(1)}, f32[256,128]{1,0:T(8,128)S(1)}) custom-call(s32[1]{0:T(128)} %bitcast.rank_ref, f32[8,1,1024]{2,1,0:T(1,128)S(1)} %bitcast.15, bf16[128,1024]{1,0:T(8,128)(2,1)S(1)} %collective-permute-done.1.refs_0_, ...), custom_call_target="tpu_custom_call" | custom-call | flops 268435456 | bytes 2097152 | tf_op jit(solution)/shard_map/normalise/pallas_call | solution.py:153
  71.9 2.9 %collective-permute-start.29 = (bf16[256,256]{1,0:T(8,128)(2,1)S(1)}, bf16[256,256]{1,0:T(8,128)(2,1)S(1)}, u32[]{:S(2)}, u32[]{:S(2)}) collective-permute-start(bf16[256,256]{1,0:T(8,128)(2,1)S(1)} %get-tuple-element.53.refs_0_), channel_id=1, source_target_pairs={{8,0},{16,8},{24,16},{0,24},{9,1},{17,9},{25,17},{1,25},{10,2},{18... | collective-permute-start | bytes 393224 | tf_op jit(solution)/shard_map/ppermute | solution.py:32
  74.8 1.1 collective-permute-start.27
  75.9 0.6 collective-permute-done.26.refs_3_
  76.6 2.9 %collective-permute-done.29.refs_6_ = bf16[256,256]{1,0:T(8,128)(2,1)S(1)} collective-permute-done((bf16[256,256]{1,0:T(8,128)(2,1)S(1)}, bf16[256,256]{1,0:T(8,128)(2,1)S(1)}, u32[]{:S(2)}, u32[]{:S(2)}) %collective-permute-start.29) | collective-permute-done | bytes 131104 | tf_op jit(solution)/shard_map/ppermute | solution.py:32
  79.5 5.3 %collective-permute-done.27.refs_4_ = bf16[256,256]{1,0:T(8,128)(2,1)S(1)} collective-permute-done((bf16[256,256]{1,0:T(8,128)(2,1)S(1)}, bf16[256,256]{1,0:T(8,128)(2,1)S(1)}, u32[]{:S(2)}, u32[]{:S(2)}) %collective-permute-start.27) | collective-permute-done | bytes 131104 | tf_op jit(solution)/shard_map/ppermute | solution.py:32
  84.8 16.0 %project.1 = (bf16[256,1024]{1,0:T(8,128)(2,1)S(1)}, bf16[256,1024]{1,0:T(8,128)(2,1)S(1)}) custom-call(s32[1]{0:T(128)} %bitcast.rank_ref, f32[256,128]{1,0:T(8,128)S(1)} %get-tuple-element.41.refs_0_, f32[256,128]{1,0:T(8,128)S(1)} %get-tuple-element.42.refs_1_, f32[256,128]{1,0:T(8,128)S(1)} %get-tuple-element.46.refs_2_, ...), custom_call_target="tpu_custom_call" | custom-call | flops 8589934592 | bytes 16777216 | tf_op jit(solution)/shard_map/project/pallas_call | solution.py:232
  100.8 8.4 %attend.3 = (bf16[256,1024]{1,0:T(8,128)(2,1)S(1)}, f32[8,1,256]{2,1,0:T(1,128)S(1)}) custom-call(s32[8]{0:T(128)S(1)} %copy-done.4, s32[1]{0:T(128)} %bitcast.1.place_ref, bf16[256,1024]{1,0:T(8,128)(2,1)S(1)} %get-tuple-element.64.q_ref, bf16[256,256]{1,0:T(8,128)(2,1)S(1)} %get-tuple-element.53.refs_0_, bf16[256,256]{1,0:T(8,128)(2,1)S(1)} %get-tuple-element.54.refs_1_, ...), custom_call_target="tpu_custom_call" | custom-call | flops 2147483648 | bytes 524288 | tf_op jit(solution)/shard_map/attend/pallas_call | solution.py:327
  109.3 4.0 %attend.2 = (bf16[256,1024]{1,0:T(8,128)(2,1)S(1)}, f32[8,1,256]{2,1,0:T(1,128)S(1)}) custom-call(s32[8]{0:T(128)S(1)} %copy-done.4, s32[1]{0:T(128)} %bitcast.1.place_ref, bf16[256,1024]{1,0:T(8,128)(2,1)S(1)} %get-tuple-element.52.q_ref, bf16[256,256]{1,0:T(8,128)(2,1)S(1)} %get-tuple-element.53.refs_0_, bf16[256,256]{1,0:T(8,128)(2,1)S(1)} %get-tuple-element.54.refs_1_, ...), custom_call_target="tpu_custom_call" | custom-call | flops 2147483648 | bytes 524288 | tf_op jit(solution)/shard_map/attend/pallas_call | solution.py:327
  113.4 0.6 collective-permute-start.31
  114.0 0.6 pad_maximum_fusion.1
  114.6 3.0 %spread.11 = (bf16[128,1024]{1,0:T(8,128)(2,1)S(1)}, bf16[128,1024]{1,0:T(8,128)(2,1)S(1)}) custom-call(s32[1]{0:T(128)} %bitcast.rank_ref, bf16[256,1024]{1,0:T(8,128)(2,1)S(1)} %get-tuple-element.65.a_ref, bf16[256,1024]{1,0:T(8,128)(2,1)S(1)} %collective-permute-done.42.b_ref, bf16[1024,8192]{1,0:T(8,128)(2,1)} %w_ref.11, ...), custom_call_target="tpu_custom_call" | custom-call | flops 1073741824 | bytes 4194304 | tf_op jit(solution)/shard_map/spread/pallas_call | solution.py:386
  117.5 0.6 collective-permute-start.44
  118.1 1.5 collective-permute-start.46
  119.6 3.0 %spread.8 = (bf16[128,1024]{1,0:T(8,128)(2,1)S(1)}, bf16[128,1024]{1,0:T(8,128)(2,1)S(1)}) custom-call(s32[1]{0:T(128)} %bitcast.rank_ref, bf16[256,1024]{1,0:T(8,128)(2,1)S(1)} %get-tuple-element.55.a_ref, bf16[256,1024]{1,0:T(8,128)(2,1)S(1)} %collective-permute-done.31.b_ref, bf16[1024,8192]{1,0:T(8,128)(2,1)} %w_ref.11, ...), custom_call_target="tpu_custom_call" | custom-call | flops 1073741824 | bytes 4194304 | tf_op jit(solution)/shard_map/spread/pallas_call | solution.py:386
  122.6 1.6 collective-permute-start.37
  124.2 0.5 collective-permute-start.39
  124.7 4.6 %spread.10 = (bf16[128,1024]{1,0:T(8,128)(2,1)S(1)}, bf16[128,1024]{1,0:T(8,128)(2,1)S(1)}, bf16[128,1024]{1,0:T(8,128)(2,1)S(1)}, bf16[128,1024]{1,0:T(8,128)(2,1)S(1)}) custom-call(s32[1]{0:T(128)} %bitcast.rank_ref, bf16[256,1024]{1,0:T(8,128)(2,1)S(1)} %get-tuple-element.65.a_ref, bf16[256,1024]{1,0:T(8,128)(2,1)S(1)} %collective-permute-done.42.b_ref, ...), custom_call_target="tpu_custom_call" | custom-call | flops 2147483648 | bytes 8388608 | tf_op jit(solution)/shard_map/spread/pallas_call | solution.py:386
  129.3 0.8 collective-permute-start.43
  130.1 3.0 %spread.9 = (bf16[128,1024]{1,0:T(8,128)(2,1)S(1)}, bf16[128,1024]{1,0:T(8,128)(2,1)S(1)}) custom-call(s32[1]{0:T(128)} %bitcast.rank_ref, bf16[256,1024]{1,0:T(8,128)(2,1)S(1)} %get-tuple-element.65.a_ref, bf16[256,1024]{1,0:T(8,128)(2,1)S(1)} %collective-permute-done.42.b_ref, bf16[1024,8192]{1,0:T(8,128)(2,1)} %w_ref.11, ...), custom_call_target="tpu_custom_call" | custom-call | flops 1073741824 | bytes 4194304 | tf_op jit(solution)/shard_map/spread/pallas_call | solution.py:386
  133.0 4.6 %spread.7 = (bf16[128,1024]{1,0:T(8,128)(2,1)S(1)}, bf16[128,1024]{1,0:T(8,128)(2,1)S(1)}, bf16[128,1024]{1,0:T(8,128)(2,1)S(1)}, bf16[128,1024]{1,0:T(8,128)(2,1)S(1)}) custom-call(s32[1]{0:T(128)} %bitcast.rank_ref, bf16[256,1024]{1,0:T(8,128)(2,1)S(1)} %get-tuple-element.55.a_ref, bf16[256,1024]{1,0:T(8,128)(2,1)S(1)} %collective-permute-done.31.b_ref, ...), custom_call_target="tpu_custom_call" | custom-call | flops 2147483648 | bytes 8388608 | tf_op jit(solution)/shard_map/spread/pallas_call | solution.py:386
  137.7 3.0 %spread.6 = (bf16[128,1024]{1,0:T(8,128)(2,1)S(1)}, bf16[128,1024]{1,0:T(8,128)(2,1)S(1)}) custom-call(s32[1]{0:T(128)} %bitcast.rank_ref, bf16[256,1024]{1,0:T(8,128)(2,1)S(1)} %get-tuple-element.55.a_ref, bf16[256,1024]{1,0:T(8,128)(2,1)S(1)} %collective-permute-done.31.b_ref, bf16[1024,8192]{1,0:T(8,128)(2,1)} %w_ref.11, ...), custom_call_target="tpu_custom_call" | custom-call | flops 1073741824 | bytes 4194304 | tf_op jit(solution)/shard_map/spread/pallas_call | solution.py:386
  140.6 1.4 collective-permute-start.48
  142.1 1.6 collective-permute-start.35
  143.8 0.6 collective-permute-start.45
  144.4 0.8 collective-permute-start.47
  145.3 1.4 collective-permute-start.41
  146.7 8.8 %collective-permute-done.45 = bf16[128,1024]{1,0:T(8,128)(2,1)S(1)} collective-permute-done((bf16[128,1024]{1,0:T(8,128)(2,1)S(1)}, bf16[128,1024]{1,0:T(8,128)(2,1)S(1)}, u32[]{:S(2)}, u32[]{:S(2)}) %collective-permute-start.45) | collective-permute-done | bytes 262176 | tf_op jit(solution)/shard_map/ppermute | solution.py:26
  155.5 1.3 collective-permute-start.38
  157.0 1.6 collective-permute-start.40
  158.7 6.3 %collective-permute-done.38 = bf16[128,1024]{1,0:T(8,128)(2,1)S(1)} collective-permute-done((bf16[128,1024]{1,0:T(8,128)(2,1)S(1)}, bf16[128,1024]{1,0:T(8,128)(2,1)S(1)}, u32[]{:S(2)}, u32[]{:S(2)}) %collective-permute-start.38) | collective-permute-done | bytes 262176 | tf_op jit(solution)/shard_map/ppermute | solution.py:26
  165.2 1.0 pad_maximum_fusion
  (85 shorter events, 2.1 us)
Async XLA Ops:
  0.6 41.4 %copy-start = (bf16[512,1024]{1,0:T(8,128)(2,1)S(1)}, bf16[512,1024]{1,0:T(8,128)(2,1)}, u32[]{:S(2)}) copy-start(bf16[512,1024]{1,0:T(8,128)(2,1)} %refs_0_.3) | copy-start | bytes 3145732
  0.6 30.2 %copy-start.4 = (s32[8]{0:T(128)S(1)}, s32[8]{0:T(128)}, u32[]{:S(2)}) copy-start(s32[8]{0:T(128)} %order_ref.3) | copy-start | bytes 100
  0.7 41.4 %copy-start.1 = (f32[8192]{0:T(1024)S(1)}, f32[8192]{0:T(1024)}, u32[]{:S(2)}) copy-start(f32[8192]{0:T(1024)} %param.8) | copy-start | bytes 98308
  1.8 17.8 %copy-start.7 = (bf16[128,1024]{1,0:T(8,128)(2,1)}, bf16[128,1024]{1,0:T(8,128)(2,1)S(1)}, u32[]{:S(2)}) copy-start(bf16[128,1024]{1,0:T(8,128)(2,1)S(1)} %get-tuple-element.83) | copy-start | bytes 786436
  1.8 10.2 %collective-permute-start = (bf16[128,1024]{1,0:T(8,128)(2,1)S(1)}, bf16[128,1024]{1,0:T(8,128)(2,1)S(1)}, u32[]{:S(2)}, u32[]{:S(2)}) collective-permute-start(bf16[128,1024]{1,0:T(8,128)(2,1)S(1)} %get-tuple-element.83), channel_id=1, source_target_pairs={{0,4},{1,5},{2,6},{3,7},{4,0},{5,1},{6,2},{7,3},{8,12},{9,13},{10,... | collective-permute-start | bytes 786440 | tf_op jit(solution)/shard_map/ppermute | solution.py:26
  4.9 12.8 %collective-permute-start.10 = (bf16[128,1024]{1,0:T(8,128)(2,1)S(1)}, bf16[128,1024]{1,0:T(8,128)(2,1)S(1)}, u32[]{:S(2)}, u32[]{:S(2)}) collective-permute-start(bf16[128,1024]{1,0:T(8,128)(2,1)S(1)} %get-tuple-element.82), channel_id=1, source_target_pairs={{0,4},{1,5},{2,6},{3,7},{4,0},{5,1},{6,2},{7,3},{8,12},{9,13},{10,... | collective-permute-start | bytes 786440 | tf_op jit(solution)/shard_map/ppermute | solution.py:26
  5.0 14.7 %collective-permute-start.2 = (bf16[128,1024]{1,0:T(8,128)(2,1)S(1)}, bf16[128,1024]{1,0:T(8,128)(2,1)S(1)}, u32[]{:S(2)}, u32[]{:S(2)}) collective-permute-start(bf16[128,1024]{1,0:T(8,128)(2,1)S(1)} %get-tuple-element.82), channel_id=1, source_target_pairs={{0,2},{1,3},{2,0},{3,1},{4,6},{5,7},{6,4},{7,5},{8,10},{9,11},{10,... | collective-permute-start | bytes 786440 | tf_op jit(solution)/shard_map/ppermute | solution.py:26
  6.9 35.1 %collective-permute-start.6 = (bf16[512,1024]{1,0:T(8,128)(2,1)}, bf16[512,1024]{1,0:T(8,128)(2,1)}, u32[]{:S(2)}, u32[]{:S(2)}) collective-permute-start(bf16[512,1024]{1,0:T(8,128)(2,1)} %refs_0_.3), channel_id=1, source_target_pairs={{0,1},{1,0},{2,3},{3,2},{4,5},{5,4},{6,7},{7,6},{8,9},{9,8},{10,11... | collective-permute-start | bytes 3145736 | tf_op jit(solution)/shard_map/ppermute | solution.py:26
  13.8 8.2 %collective-permute-start.15 = (bf16[128,1024]{1,0:T(8,128)(2,1)S(1)}, bf16[128,1024]{1,0:T(8,128)(2,1)S(1)}, u32[]{:S(2)}, u32[]{:S(2)}) collective-permute-start(bf16[128,1024]{1,0:T(8,128)(2,1)S(1)} %get-tuple-element.80), channel_id=1, source_target_pairs={{0,2},{1,3},{2,0},{3,1},{4,6},{5,7},{6,4},{7,5},{8,10},{9,11},{10,... | collective-permute-start | bytes 786440 | tf_op jit(solution)/shard_map/ppermute | solution.py:26
  15.8 9.0 %collective-permute-start.22 = (bf16[128,1024]{1,0:T(8,128)(2,1)S(1)}, bf16[128,1024]{1,0:T(8,128)(2,1)S(1)}, u32[]{:S(2)}, u32[]{:S(2)}) collective-permute-start(bf16[128,1024]{1,0:T(8,128)(2,1)S(1)} %get-tuple-element.80), channel_id=1, source_target_pairs={{0,4},{1,5},{2,6},{3,7},{4,0},{5,1},{6,2},{7,3},{8,12},{9,13},{10,... | collective-permute-start | bytes 786440 | tf_op jit(solution)/shard_map/ppermute | solution.py:26
  17.7 8.9 %collective-permute-start.19 = (bf16[128,1024]{1,0:T(8,128)(2,1)}, bf16[128,1024]{1,0:T(8,128)(2,1)S(1)}, u32[]{:S(2)}, u32[]{:S(2)}) collective-permute-start(bf16[128,1024]{1,0:T(8,128)(2,1)} %get-tuple-element.81), channel_id=1, source_target_pairs={{0,2},{1,3},{2,0},{3,1},{4,6},{5,7},{6,4},{7,5},{8,10},{9,11},{10,... | collective-permute-start | bytes 786440 | tf_op jit(solution)/shard_map/ppermute | solution.py:26
  19.7 10.8 %collective-permute-start.13 = (bf16[128,1024]{1,0:T(8,128)(2,1)}, bf16[128,1024]{1,0:T(8,128)(2,1)S(1)}, u32[]{:S(2)}, u32[]{:S(2)}) collective-permute-start(bf16[128,1024]{1,0:T(8,128)(2,1)} %get-tuple-element.81), channel_id=1, source_target_pairs={{0,4},{1,5},{2,6},{3,7},{4,0},{5,1},{6,2},{7,3},{8,12},{9,13},{10,... | collective-permute-start | bytes 786440 | tf_op jit(solution)/shard_map/ppermute | solution.py:26
  22.0 9.8 %collective-permute-start.21 = (bf16[128,1024]{1,0:T(8,128)(2,1)S(1)}, bf16[128,1024]{1,0:T(8,128)(2,1)S(1)}, u32[]{:S(2)}, u32[]{:S(2)}) collective-permute-start(bf16[128,1024]{1,0:T(8,128)(2,1)S(1)} %collective-permute-done.15.refs_3_), channel_id=1, source_target_pairs={{0,1},{1,0},{2,3},{3,2},{4,5},{5,4},{6,7},{7,6},{8,9},{9,8},{10,11... | collective-permute-start | bytes 786440 | tf_op jit(solution)/shard_map/ppermute | solution.py:26
  24.8 8.8 %collective-permute-start.16 = (bf16[128,1024]{1,0:T(8,128)(2,1)S(1)}, bf16[128,1024]{1,0:T(8,128)(2,1)S(1)}, u32[]{:S(2)}, u32[]{:S(2)}) collective-permute-start(bf16[128,1024]{1,0:T(8,128)(2,1)S(1)} %collective-permute-done.15.refs_3_), channel_id=1, source_target_pairs={{0,4},{1,5},{2,6},{3,7},{4,0},{5,1},{6,2},{7,3},{8,12},{9,13},{10,... | collective-permute-start | bytes 786440 | tf_op jit(solution)/shard_map/ppermute | solution.py:26
  26.5 4.5 %collective-permute-start.24 = (bf16[128,1024]{1,0:T(8,128)(2,1)S(1)}, bf16[128,1024]{1,0:T(8,128)(2,1)S(1)}, u32[]{:S(2)}, u32[]{:S(2)}) collective-permute-start(bf16[128,1024]{1,0:T(8,128)(2,1)S(1)} %collective-permute-done.22.refs_7_), channel_id=1, source_target_pairs={{0,1},{1,0},{2,3},{3,2},{4,5},{5,4},{6,7},{7,6},{8,9},{9,8},{10,11... | collective-permute-start | bytes 786440 | tf_op jit(solution)/shard_map/ppermute | solution.py:26
  30.4 6.5 %collective-permute-start.14 = (bf16[128,1024]{1,0:T(8,128)(2,1)S(1)}, bf16[128,1024]{1,0:T(8,128)(2,1)}, u32[]{:S(2)}, u32[]{:S(2)}) collective-permute-start(bf16[128,1024]{1,0:T(8,128)(2,1)S(1)} %collective-permute-done.13.refs_6_), channel_id=1, source_target_pairs={{0,2},{1,3},{2,0},{3,1},{4,6},{5,7},{6,4},{7,5},{8,10},{9,11},{10,... | collective-permute-start | bytes 786440 | tf_op jit(solution)/shard_map/ppermute | solution.py:26
  31.0 0.7 copy-start.2
  31.8 6.8 %collective-permute-start.23 = (bf16[128,1024]{1,0:T(8,128)(2,1)S(1)}, bf16[128,1024]{1,0:T(8,128)(2,1)}, u32[]{:S(2)}, u32[]{:S(2)}) collective-permute-start(bf16[128,1024]{1,0:T(8,128)(2,1)S(1)} %collective-permute-done.13.refs_6_), channel_id=1, source_target_pairs={{0,1},{1,0},{2,3},{3,2},{4,5},{5,4},{6,7},{7,6},{8,9},{9,8},{10,11... | collective-permute-start | bytes 786440 | tf_op jit(solution)/shard_map/ppermute | solution.py:26
  31.8 6.2 %collective-permute-start.20 = (bf16[128,1024]{1,0:T(8,128)(2,1)S(1)}, bf16[128,1024]{1,0:T(8,128)(2,1)}, u32[]{:S(2)}, u32[]{:S(2)}) collective-permute-start(bf16[128,1024]{1,0:T(8,128)(2,1)S(1)} %collective-permute-done.19.refs_2_), channel_id=1, source_target_pairs={{0,1},{1,0},{2,3},{3,2},{4,5},{5,4},{6,7},{7,6},{8,9},{9,8},{10,11... | collective-permute-start | bytes 786440 | tf_op jit(solution)/shard_map/ppermute | solution.py:26
  33.7 5.0 %collective-permute-start.18 = (bf16[128,1024]{1,0:T(8,128)(2,1)S(1)}, bf16[128,1024]{1,0:T(8,128)(2,1)}, u32[]{:S(2)}, u32[]{:S(2)}) collective-permute-start(bf16[128,1024]{1,0:T(8,128)(2,1)S(1)} %collective-permute-done.16.refs_1_), channel_id=1, source_target_pairs={{0,1},{1,0},{2,3},{3,2},{4,5},{5,4},{6,7},{7,6},{8,9},{9,8},{10,11... | collective-permute-start | bytes 786440 | tf_op jit(solution)/shard_map/ppermute | solution.py:26
  36.9 3.5 %collective-permute-start.17 = (bf16[128,1024]{1,0:T(8,128)(2,1)}, bf16[128,1024]{1,0:T(8,128)(2,1)}, u32[]{:S(2)}, u32[]{:S(2)}) collective-permute-start(bf16[128,1024]{1,0:T(8,128)(2,1)} %collective-permute-done.14.refs_0_), channel_id=1, source_target_pairs={{0,1},{1,0},{2,3},{3,2},{4,5},{5,4},{6,7},{7,6},{8,9},{9,8},{10,11... | collective-permute-start | bytes 786440 | tf_op jit(solution)/shard_map/ppermute | solution.py:26
  38.0 12.3 %collective-permute-start.7 = (bf16[128,1024]{1,0:T(8,128)(2,1)}, bf16[128,1024]{1,0:T(8,128)(2,1)S(1)}, u32[]{:S(2)}, u32[]{:S(2)}) collective-permute-start(bf16[128,1024]{1,0:T(8,128)(2,1)} %copy-done.7), channel_id=1, source_target_pairs={{0,2},{1,3},{2,0},{3,1},{4,6},{5,7},{6,4},{7,5},{8,10},{9,11},{10,... | collective-permute-start | bytes 786440 | tf_op jit(solution)/shard_map/ppermute | solution.py:26
  38.5 14.0 %collective-permute-start.9 = (bf16[128,1024]{1,0:T(8,128)(2,1)S(1)}, bf16[128,1024]{1,0:T(8,128)(2,1)S(1)}, u32[]{:S(2)}, u32[]{:S(2)}) collective-permute-start(bf16[128,1024]{1,0:T(8,128)(2,1)S(1)} %collective-permute-done.2.refs_3_), channel_id=1, source_target_pairs={{0,1},{1,0},{2,3},{3,2},{4,5},{5,4},{6,7},{7,6},{8,9},{9,8},{10,11... | collective-permute-start | bytes 786440 | tf_op jit(solution)/shard_map/ppermute | solution.py:26
  38.7 12.2 %collective-permute-start.3 = (bf16[128,1024]{1,0:T(8,128)(2,1)S(1)}, bf16[128,1024]{1,0:T(8,128)(2,1)S(1)}, u32[]{:S(2)}, u32[]{:S(2)}) collective-permute-start(bf16[128,1024]{1,0:T(8,128)(2,1)S(1)} %collective-permute-done.2.refs_3_), channel_id=1, source_target_pairs={{0,4},{1,5},{2,6},{3,7},{4,0},{5,1},{6,2},{7,3},{8,12},{9,13},{10,... | collective-permute-start | bytes 786440 | tf_op jit(solution)/shard_map/ppermute | solution.py:26
  40.5 12.1 %collective-permute-start.1 = (bf16[128,1024]{1,0:T(8,128)(2,1)S(1)}, bf16[128,1024]{1,0:T(8,128)(2,1)S(1)}, u32[]{:S(2)}, u32[]{:S(2)}) collective-permute-start(bf16[128,1024]{1,0:T(8,128)(2,1)S(1)} %collective-permute-done.refs_6_), channel_id=1, source_target_pairs={{0,2},{1,3},{2,0},{3,1},{4,6},{5,7},{6,4},{7,5},{8,10},{9,11},{10,... | collective-permute-start | bytes 786440 | tf_op jit(solution)/shard_map/ppermute | solution.py:26
  42.0 8.9 %collective-permute-start.12 = (bf16[128,1024]{1,0:T(8,128)(2,1)S(1)}, bf16[128,1024]{1,0:T(8,128)(2,1)S(1)}, u32[]{:S(2)}, u32[]{:S(2)}) collective-permute-start(bf16[128,1024]{1,0:T(8,128)(2,1)S(1)} %collective-permute-done.10.refs_7_), channel_id=1, source_target_pairs={{0,1},{1,0},{2,3},{3,2},{4,5},{5,4},{6,7},{7,6},{8,9},{9,8},{10,11... | collective-permute-start | bytes 786440 | tf_op jit(solution)/shard_map/ppermute | solution.py:26
  42.0 1.0 copy-start.3
  50.3 13.3 %collective-permute-start.11 = (bf16[128,1024]{1,0:T(8,128)(2,1)S(1)}, bf16[128,1024]{1,0:T(8,128)(2,1)S(1)}, u32[]{:S(2)}, u32[]{:S(2)}) collective-permute-start(bf16[128,1024]{1,0:T(8,128)(2,1)S(1)} %collective-permute-done.refs_6_), channel_id=1, source_target_pairs={{0,1},{1,0},{2,3},{3,2},{4,5},{5,4},{6,7},{7,6},{8,9},{9,8},{10,11... | collective-permute-start | bytes 786440 | tf_op jit(solution)/shard_map/ppermute | solution.py:26
  50.8 12.5 %collective-permute-start.8 = (bf16[128,1024]{1,0:T(8,128)(2,1)S(1)}, bf16[128,1024]{1,0:T(8,128)(2,1)S(1)}, u32[]{:S(2)}, u32[]{:S(2)}) collective-permute-start(bf16[128,1024]{1,0:T(8,128)(2,1)S(1)} %collective-permute-done.7.refs_2_), channel_id=1, source_target_pairs={{0,1},{1,0},{2,3},{3,2},{4,5},{5,4},{6,7},{7,6},{8,9},{9,8},{10,11... | collective-permute-start | bytes 786440 | tf_op jit(solution)/shard_map/ppermute | solution.py:26
  50.9 17.8 %collective-permute-start.5 = (bf16[128,1024]{1,0:T(8,128)(2,1)S(1)}, bf16[128,1024]{1,0:T(8,128)(2,1)S(1)}, u32[]{:S(2)}, u32[]{:S(2)}) collective-permute-start(bf16[128,1024]{1,0:T(8,128)(2,1)S(1)} %collective-permute-done.3.refs_1_), channel_id=1, source_target_pairs={{0,1},{1,0},{2,3},{3,2},{4,5},{5,4},{6,7},{7,6},{8,9},{9,8},{10,11... | collective-permute-start | bytes 786440 | tf_op jit(solution)/shard_map/ppermute | solution.py:26
  52.6 17.2 %collective-permute-start.4 = (bf16[128,1024]{1,0:T(8,128)(2,1)S(1)}, bf16[128,1024]{1,0:T(8,128)(2,1)S(1)}, u32[]{:S(2)}, u32[]{:S(2)}) collective-permute-start(bf16[128,1024]{1,0:T(8,128)(2,1)S(1)} %collective-permute-done.1.refs_0_), channel_id=1, source_target_pairs={{0,1},{1,0},{2,3},{3,2},{4,5},{5,4},{6,7},{7,6},{8,9},{9,8},{10,11... | collective-permute-start | bytes 786440 | tf_op jit(solution)/shard_map/ppermute | solution.py:26
  52.6 22.2 %collective-permute-start.30 = (bf16[256,256]{1,0:T(8,128)(2,1)S(1)}, bf16[256,256]{1,0:T(8,128)(2,1)S(1)}, u32[]{:S(2)}, u32[]{:S(2)}) collective-permute-start(bf16[256,256]{1,0:T(8,128)(2,1)S(1)} %get-tuple-element.54.refs_1_), channel_id=1, source_target_pairs={{8,0},{16,8},{24,16},{0,24},{9,1},{17,9},{25,17},{1,25},{10,2},{18... | collective-permute-start | bytes 393224 | tf_op jit(solution)/shard_map/ppermute | solution.py:32
  63.4 51.2 %collective-permute-start.36 = (bf16[1024,1024]{1,0:T(8,128)(2,1)}, bf16[1024,1024]{1,0:T(8,128)(2,1)S(1)}, u32[]{:S(2)}, u32[]{:S(2)}) collective-permute-start(bf16[1024,1024]{1,0:T(8,128)(2,1)} %get-tuple-element.77), channel_id=1, source_target_pairs={{0,1},{1,0},{2,3},{3,2},{4,5},{5,4},{6,7},{7,6},{8,9},{9,8},{10,11... | collective-permute-start | bytes 6291464 | tf_op jit(solution)/shard_map/ppermute | solution.py:26
  63.6 12.3 %collective-permute-start.28 = (bf16[256,256]{1,0:T(8,128)(2,1)S(1)}, bf16[256,256]{1,0:T(8,128)(2,1)S(1)}, u32[]{:S(2)}, u32[]{:S(2)}) collective-permute-start(bf16[256,256]{1,0:T(8,128)(2,1)S(1)} %get-tuple-element.54.refs_1_), channel_id=1, source_target_pairs={{16,0},{24,8},{0,16},{8,24},{17,1},{25,9},{1,17},{9,25},{18,2},{26... | collective-permute-start | bytes 393224 | tf_op jit(solution)/shard_map/ppermute | solution.py:32
  68.7 7.8 %collective-permute-start.26 = (bf16[256,256]{1,0:T(8,128)(2,1)S(1)}, bf16[256,256]{1,0:T(8,128)(2,1)S(1)}, u32[]{:S(2)}, u32[]{:S(2)}) collective-permute-start(bf16[256,256]{1,0:T(8,128)(2,1)S(1)} %get-tuple-element.54.refs_1_), channel_id=1, source_target_pairs={{24,0},{0,8},{8,16},{16,24},{25,1},{1,9},{9,17},{17,25},{26,2},{2,... | collective-permute-start | bytes 393224 | tf_op jit(solution)/shard_map/ppermute | solution.py:32
  69.8 9.7 %copy-start.6 = (bf16[1024,1024]{1,0:T(8,128)(2,1)S(1)}, bf16[1024,1024]{1,0:T(8,128)(2,1)}, u32[]{:S(2)}) copy-start(bf16[1024,1024]{1,0:T(8,128)(2,1)} %get-tuple-element.79) | copy-start | bytes 6291460
  71.9 7.5 %collective-permute-start.29 = (bf16[256,256]{1,0:T(8,128)(2,1)S(1)}, bf16[256,256]{1,0:T(8,128)(2,1)S(1)}, u32[]{:S(2)}, u32[]{:S(2)}) collective-permute-start(bf16[256,256]{1,0:T(8,128)(2,1)S(1)} %get-tuple-element.53.refs_0_), channel_id=1, source_target_pairs={{8,0},{16,8},{24,16},{0,24},{9,1},{17,9},{25,17},{1,25},{10,2},{18... | collective-permute-start | bytes 393224 | tf_op jit(solution)/shard_map/ppermute | solution.py:32
  74.8 10.0 %collective-permute-start.27 = (bf16[256,256]{1,0:T(8,128)(2,1)S(1)}, bf16[256,256]{1,0:T(8,128)(2,1)S(1)}, u32[]{:S(2)}, u32[]{:S(2)}) collective-permute-start(bf16[256,256]{1,0:T(8,128)(2,1)S(1)} %get-tuple-element.53.refs_0_), channel_id=1, source_target_pairs={{16,0},{24,8},{0,16},{8,24},{17,1},{25,9},{1,17},{9,25},{18,2},{26... | collective-permute-start | bytes 393224 | tf_op jit(solution)/shard_map/ppermute | solution.py:32
  75.9 53.4 %collective-permute-start.32 = (bf16[1024,1024]{1,0:T(8,128)(2,1)}, bf16[1024,1024]{1,0:T(8,128)(2,1)S(1)}, u32[]{:S(2)}, u32[]{:S(2)}) collective-permute-start(bf16[1024,1024]{1,0:T(8,128)(2,1)} %get-tuple-element.76), channel_id=1, source_target_pairs={{0,1},{1,0},{2,3},{3,2},{4,5},{5,4},{6,7},{7,6},{8,9},{9,8},{10,11... | collective-permute-start | bytes 6291464 | tf_op jit(solution)/shard_map/ppermute | solution.py:26
  76.5 46.1 %collective-permute-start.34 = (bf16[1024,1024]{1,0:T(8,128)(2,1)}, bf16[1024,1024]{1,0:T(8,128)(2,1)S(1)}, u32[]{:S(2)}, u32[]{:S(2)}) collective-permute-start(bf16[1024,1024]{1,0:T(8,128)(2,1)} %get-tuple-element.78), channel_id=1, source_target_pairs={{0,1},{1,0},{2,3},{3,2},{4,5},{5,4},{6,7},{7,6},{8,9},{9,8},{10,11... | collective-permute-start | bytes 6291464 | tf_op jit(solution)/shard_map/ppermute | solution.py:26
  79.5 44.7 %collective-permute-start.33 = (bf16[1024,1024]{1,0:T(8,128)(2,1)S(1)}, bf16[1024,1024]{1,0:T(8,128)(2,1)}, u32[]{:S(2)}, u32[]{:S(2)}) collective-permute-start(bf16[1024,1024]{1,0:T(8,128)(2,1)S(1)} %copy-done.6), channel_id=1, source_target_pairs={{0,1},{1,0},{2,3},{3,2},{4,5},{5,4},{6,7},{7,6},{8,9},{9,8},{10,11... | collective-permute-start | bytes 6291464 | tf_op jit(solution)/shard_map/ppermute | solution.py:26
  84.8 16.0 %collective-permute-start.25 = (bf16[256,256]{1,0:T(8,128)(2,1)S(1)}, bf16[256,256]{1,0:T(8,128)(2,1)S(1)}, u32[]{:S(2)}, u32[]{:S(2)}) collective-permute-start(bf16[256,256]{1,0:T(8,128)(2,1)S(1)} %get-tuple-element.53.refs_0_), channel_id=1, source_target_pairs={{24,0},{0,8},{8,16},{16,24},{25,1},{1,9},{9,17},{17,25},{26,2},{2,... | collective-permute-start | bytes 393224 | tf_op jit(solution)/shard_map/ppermute | solution.py:32
  109.3 4.1 %collective-permute-start.42 = (bf16[256,1024]{1,0:T(8,128)(2,1)S(1)}, bf16[256,1024]{1,0:T(8,128)(2,1)S(1)}, u32[]{:S(2)}, u32[]{:S(2)}) collective-permute-start(bf16[256,1024]{1,0:T(8,128)(2,1)S(1)} %get-tuple-element.65.a_ref), channel_id=1, source_target_pairs={{0,1},{1,0},{2,3},{3,2},{4,5},{5,4},{6,7},{7,6},{8,9},{9,8},{10,11... | collective-permute-start | bytes 1572872 | tf_op jit(solution)/shard_map/ppermute | solution.py:26
  113.4 4.7 %collective-permute-start.31 = (bf16[256,1024]{1,0:T(8,128)(2,1)S(1)}, bf16[256,1024]{1,0:T(8,128)(2,1)S(1)}, u32[]{:S(2)}, u32[]{:S(2)}) collective-permute-start(bf16[256,1024]{1,0:T(8,128)(2,1)S(1)} %get-tuple-element.55.a_ref), channel_id=1, source_target_pairs={{0,1},{1,0},{2,3},{3,2},{4,5},{5,4},{6,7},{7,6},{8,9},{9,8},{10,11... | collective-permute-start | bytes 1572872 | tf_op jit(solution)/shard_map/ppermute | solution.py:26
  117.5 24.6 %collective-permute-start.44 = (bf16[128,1024]{1,0:T(8,128)(2,1)S(1)}, bf16[128,1024]{1,0:T(8,128)(2,1)S(1)}, u32[]{:S(2)}, u32[]{:S(2)}) collective-permute-start(bf16[128,1024]{1,0:T(8,128)(2,1)S(1)} %get-tuple-element.69), channel_id=1, source_target_pairs={{0,2},{1,3},{2,0},{3,1},{4,6},{5,7},{6,4},{7,5},{8,10},{9,11},{10,... | collective-permute-start | bytes 786440 | tf_op jit(solution)/shard_map/ppermute | solution.py:26
  118.1 25.6 %collective-permute-start.46 = (bf16[128,1024]{1,0:T(8,128)(2,1)S(1)}, bf16[128,1024]{1,0:T(8,128)(2,1)S(1)}, u32[]{:S(2)}, u32[]{:S(2)}) collective-permute-start(bf16[128,1024]{1,0:T(8,128)(2,1)S(1)} %get-tuple-element.72), channel_id=1, source_target_pairs={{0,4},{1,5},{2,6},{3,7},{4,0},{5,1},{6,2},{7,3},{8,12},{9,13},{10,... | collective-permute-start | bytes 786440 | tf_op jit(solution)/shard_map/ppermute | solution.py:26
  122.6 2.1 %copy-start.5 = (bf16[1024,1024]{1,0:T(8,128)(2,1)}, bf16[1024,1024]{1,0:T(8,128)(2,1)S(1)}, u32[]{:S(2)}) copy-start(bf16[1024,1024]{1,0:T(8,128)(2,1)S(1)} %collective-permute-done.34.refs_1_) | copy-start | bytes 6291460
  122.6 21.8 %collective-permute-start.37 = (bf16[128,1024]{1,0:T(8,128)(2,1)S(1)}, bf16[128,1024]{1,0:T(8,128)(2,1)S(1)}, u32[]{:S(2)}, u32[]{:S(2)}) collective-permute-start(bf16[128,1024]{1,0:T(8,128)(2,1)S(1)} %get-tuple-element.59), channel_id=1, source_target_pairs={{0,2},{1,3},{2,0},{3,1},{4,6},{5,7},{6,4},{7,5},{8,10},{9,11},{10,... | collective-permute-start | bytes 786440 | tf_op jit(solution)/shard_map/ppermute | solution.py:26
  124.2 16.4 %collective-permute-start.39 = (bf16[128,1024]{1,0:T(8,128)(2,1)S(1)}, bf16[128,1024]{1,0:T(8,128)(2,1)S(1)}, u32[]{:S(2)}, u32[]{:S(2)}) collective-permute-start(bf16[128,1024]{1,0:T(8,128)(2,1)S(1)} %get-tuple-element.62), channel_id=1, source_target_pairs={{0,4},{1,5},{2,6},{3,7},{4,0},{5,1},{6,2},{7,3},{8,12},{9,13},{10,... | collective-permute-start | bytes 786440 | tf_op jit(solution)/shard_map/ppermute | solution.py:26
  129.3 15.9 %collective-permute-start.43 = (bf16[128,1024]{1,0:T(8,128)(2,1)S(1)}, bf16[128,1024]{1,0:T(8,128)(2,1)S(1)}, u32[]{:S(2)}, u32[]{:S(2)}) collective-permute-start(bf16[128,1024]{1,0:T(8,128)(2,1)S(1)} %get-tuple-element.67), channel_id=1, source_target_pairs={{0,2},{1,3},{2,0},{3,1},{4,6},{5,7},{6,4},{7,5},{8,10},{9,11},{10,... | collective-permute-start | bytes 786440 | tf_op jit(solution)/shard_map/ppermute | solution.py:26
  140.6 16.3 %collective-permute-start.48 = (bf16[128,1024]{1,0:T(8,128)(2,1)S(1)}, bf16[128,1024]{1,0:T(8,128)(2,1)S(1)}, u32[]{:S(2)}, u32[]{:S(2)}) collective-permute-start(bf16[128,1024]{1,0:T(8,128)(2,1)S(1)} %get-tuple-element.73), channel_id=1, source_target_pairs={{0,4},{1,5},{2,6},{3,7},{4,0},{5,1},{6,2},{7,3},{8,12},{9,13},{10,... | collective-permute-start | bytes 786440 | tf_op jit(solution)/shard_map/ppermute | solution.py:26
  142.1 16.6 %collective-permute-start.35 = (bf16[128,1024]{1,0:T(8,128)(2,1)S(1)}, bf16[128,1024]{1,0:T(8,128)(2,1)S(1)}, u32[]{:S(2)}, u32[]{:S(2)}) collective-permute-start(bf16[128,1024]{1,0:T(8,128)(2,1)S(1)} %get-tuple-element.57), channel_id=1, source_target_pairs={{0,2},{1,3},{2,0},{3,1},{4,6},{5,7},{6,4},{7,5},{8,10},{9,11},{10,... | collective-permute-start | bytes 786440 | tf_op jit(solution)/shard_map/ppermute | solution.py:26
  143.8 11.7 %collective-permute-start.45 = (bf16[128,1024]{1,0:T(8,128)(2,1)S(1)}, bf16[128,1024]{1,0:T(8,128)(2,1)S(1)}, u32[]{:S(2)}, u32[]{:S(2)}) collective-permute-start(bf16[128,1024]{1,0:T(8,128)(2,1)S(1)} %add_convert_fusion.3), channel_id=1, source_target_pairs={{0,4},{1,5},{2,6},{3,7},{4,0},{5,1},{6,2},{7,3},{8,12},{9,13},{10,... | collective-permute-start | bytes 786440 | tf_op jit(solution)/shard_map/ppermute | solution.py:26
  144.4 14.1 %collective-permute-start.47 = (bf16[128,1024]{1,0:T(8,128)(2,1)S(1)}, bf16[128,1024]{1,0:T(8,128)(2,1)S(1)}, u32[]{:S(2)}, u32[]{:S(2)}) collective-permute-start(bf16[128,1024]{1,0:T(8,128)(2,1)S(1)} %add_convert_fusion.1), channel_id=1, source_target_pairs={{0,2},{1,3},{2,0},{3,1},{4,6},{5,7},{6,4},{7,5},{8,10},{9,11},{10,... | collective-permute-start | bytes 786440 | tf_op jit(solution)/shard_map/ppermute | solution.py:26
  145.3 19.8 %collective-permute-start.41 = (bf16[128,1024]{1,0:T(8,128)(2,1)S(1)}, bf16[128,1024]{1,0:T(8,128)(2,1)S(1)}, u32[]{:S(2)}, u32[]{:S(2)}) collective-permute-start(bf16[128,1024]{1,0:T(8,128)(2,1)S(1)} %get-tuple-element.63), channel_id=1, source_target_pairs={{0,4},{1,5},{2,6},{3,7},{4,0},{5,1},{6,2},{7,3},{8,12},{9,13},{10,... | collective-permute-start | bytes 786440 | tf_op jit(solution)/shard_map/ppermute | solution.py:26
  155.5 9.5 %collective-permute-start.38 = (bf16[128,1024]{1,0:T(8,128)(2,1)S(1)}, bf16[128,1024]{1,0:T(8,128)(2,1)S(1)}, u32[]{:S(2)}, u32[]{:S(2)}) collective-permute-start(bf16[128,1024]{1,0:T(8,128)(2,1)S(1)} %add_convert_fusion.7), channel_id=1, source_target_pairs={{0,4},{1,5},{2,6},{3,7},{4,0},{5,1},{6,2},{7,3},{8,12},{9,13},{10,... | collective-permute-start | bytes 786440 | tf_op jit(solution)/shard_map/ppermute | solution.py:26
  157.0 8.1 %collective-permute-start.40 = (bf16[128,1024]{1,0:T(8,128)(2,1)S(1)}, bf16[128,1024]{1,0:T(8,128)(2,1)S(1)}, u32[]{:S(2)}, u32[]{:S(2)}) collective-permute-start(bf16[128,1024]{1,0:T(8,128)(2,1)S(1)} %add_convert_fusion.5), channel_id=1, source_target_pairs={{0,2},{1,3},{2,0},{3,1},{4,6},{5,7},{6,4},{7,5},{8,10},{9,11},{10,... | collective-permute-start | bytes 786440 | tf_op jit(solution)/shard_map/ppermute | solution.py:26
